TPU v7x, 256 devices: a whole 4x4x8 slice. The times are simulated.
256 devices in a mesh: dp: 32 (over z, y), mp: 8 (over x, core).
Axes of the slice: x: 4, y: 4, z: 8, core: 2. Of those that a mesh axis runs over, the one named last changes fastest.
Arguments:
- queries: bfloat16 [512, 8192], P('dp', 'mp'), may hold values from -8 to 8
- incoming_key: bfloat16 [512, 1024], P('dp', 'mp'), may hold values from -4 to 4
- incoming_value: bfloat16 [512, 1024], P('dp', 'mp'), may hold values from -4 to 4
- key_cache: bfloat16 [1024, 256, 1024], P('dp', None, 'mp'), may hold values from -8 to 8
- cached_values: bfloat16 [1024, 256, 1024], P('dp', None, 'mp'), may hold values from -4 to 4
- task_key_scale: bfloat16 [256, 1024], P(None, 'mp'), may hold values from 0.099609375 to 1.8984375
- task_value_scale: bfloat16 [256, 1024], P(None, 'mp'), may hold values from 0.099609375 to 1.8984375
- out_weight: bfloat16 [8192, 8192], P('mp', 'dp'), may hold values from -0.0625 to 0.0625
- task_id: int32 [512], P('dp'), may hold values from 0 to 255, as said below
- cached_length: int32 [512], P('dp'), may hold values from 1 to 256, as said below
- task_owner: int32 [256], replicated, may hold values from 0 to 31, as said below
- cache_slot: int32 [512], P('dp'), may hold values from 0 to 31, as said below
Outputs:
- layer_out: bfloat16 [512, 8192], P('dp', 'mp')
Inputs may be any that keep to these rules, and one draw needn't show every extreme that they name: `task_owner`: every dp index owns the same number of tasks. `task_id`: among the 16 requests of one dp index at most 1 have tasks of one owner; in every draw one owner gets exactly 1 from every dp index. `cache_slot`: requests of one owner have distinct slots; one owner uses all 32. `cached_length`: every dp index has a request with 256 cached positions.
All inputs are finite; a program needn't handle non-finite values.
Results may differ from a plain program's by a relative error of at most 0.0073.
Values may be sent and summed in bfloat16 or wider, within the bound.
A program may use at most 128 MiB of HBM per device.

v0:
```python
import functools
import math

import jax
import jax.numpy as jnp
from jax import lax
from jax.experimental import pallas as pl
from jax.experimental.pallas import tpu as pltpu
from jax.sharding import PartitionSpec as P

KEY_VALUE_HEADS = 8
HEAD_SIZE = 128
QUERY_HEADS = 64
GROUP = QUERY_HEADS // KEY_VALUE_HEADS
META = 128
FIRST = 16
TOGETHER = 8
CHUNKS = 4
MESH = pl.DeviceIdType.MESH

masked_score = -1e30
f32 = jnp.float32
bf16 = jnp.bfloat16


def iota(shape, dim):
    return lax.broadcasted_iota(jnp.int32, shape, dim)


def to_column(row):
    n = row.shape[1]
    eye = iota((n, n), 0) == iota((n, n), 1)
    return jnp.sum(jnp.where(eye, row, 0.0), axis=1, keepdims=True)


def to_row(column):
    n = column.shape[0]
    eye = iota((n, n), 0) == iota((n, n), 1)
    return jnp.sum(jnp.where(eye, column, 0.0), axis=0, keepdims=True)


def factors(dp):
    inner = 2 ** (int(math.log2(dp)) // 2)
    return dp // inner, inner


def dot(a, b):
    return jnp.dot(a, b, preferred_element_type=f32)


def layer_kernel(
    dp,
    mp,
    query_ref,
    new_key_ref,
    new_value_ref,
    key_scale_ref,
    value_scale_ref,
    task_ref,
    length_ref,
    slot_ref,
    owner_ref,
    key_hbm,
    value_hbm,
    weight_hbm,
    out_ref,
    keys,
    values,
    weight,
    rows_f32,
    send_rows,
    recv_rows,
    slot_query,
    slot_small,
    slot_length,
    slot_context,
    context,
    selector,
    send_part,
    recv_part,
    local_sem,
    send_sem,
    recv_sem,
    along_send,
    along_recv,
    across_send,
    across_recv,
):
    me = lax.axis_index("dp")
    part = lax.axis_index("mp")
    rows, query_width = query_ref.shape
    kv_width = new_key_ref.shape[1]
    kv_heads = kv_width // HEAD_SIZE
    heads = kv_heads * GROUP
    task_total = key_scale_ref.shape[0]
    slots, positions, _ = keys.shape
    capacity = send_rows.shape[1]
    items = dp * capacity
    columns = weight.shape[1]
    blocks = dp // mp
    meta_at = query_width + 2 * kv_width
    chunks, chunk = context.shape[1:3]
    outer, inner = factors(dp)

    total = dp * mp
    here = me * mp + part
    barrier = pltpu.get_barrier_semaphore()

    def greet(k, carry):
        other = lax.rem(here + k, total)
        pl.semaphore_signal(
            barrier,
            inc=1,
            device_id=(other // mp, lax.rem(other, mp)),
            device_id_type=MESH,
        )
        return carry

    lax.fori_loop(1, total, greet, 0)

    fetches = [
        pltpu.make_async_copy(key_hbm, keys, local_sem.at[0]),
        pltpu.make_async_copy(value_hbm, values, local_sem.at[1]),
        pltpu.make_async_copy(weight_hbm, weight, local_sem.at[2]),
    ]
    for fetch in fetches:
        fetch.start()

    task_column = to_column(task_ref[...].astype(f32))
    length_column = to_column(length_ref[...].astype(f32))
    slot_column = to_column(slot_ref[...].astype(f32))
    picked = task_column == iota((rows, task_total), 1).astype(f32)
    owner_column = jnp.sum(
        jnp.where(picked, owner_ref[...].astype(f32), 0.0), axis=1, keepdims=True
    )
    owner_row = to_row(owner_column)
    earlier = iota((rows, rows), 1) < iota((rows, rows), 0)
    rank = jnp.sum(
        jnp.where(earlier & (owner_column == owner_row), 1.0, 0.0), axis=1, keepdims=True
    )
    position_row = to_row(owner_column * capacity + rank)
    packer = jnp.where(position_row == iota((items, rows), 0).astype(f32), 1.0, 0.0).astype(bf16)
    key_factor = dot(jnp.where(picked, 1.0, 0.0).astype(bf16), key_scale_ref[...])
    for h in range(heads):
        g = h // GROUP
        lanes = slice(h * HEAD_SIZE, (h + 1) * HEAD_SIZE)
        scaled = (
            query_ref[:, lanes].astype(f32) * key_factor[:, g * HEAD_SIZE : (g + 1) * HEAD_SIZE]
        ).astype(bf16)
        rows_f32[:, lanes] = dot(packer, scaled)
    rows_f32[:, query_width : query_width + kv_width] = dot(packer, new_key_ref[...])
    rows_f32[:, query_width + kv_width : meta_at] = dot(packer, new_value_ref[...])
    lane = iota((rows, META), 1)
    line = iota((rows, META), 0)
    task_high = jnp.floor(task_column * (1.0 / 128.0))
    task_low = task_column - task_high * 128.0
    facts = (
        jnp.where(lane == 0, slot_column + 1.0, 0.0)
        + jnp.where(lane == 1, length_column, 0.0)
        + jnp.where(lane == 2, task_high, 0.0)
        + jnp.where(lane == 3, task_low, 0.0)
    )
    shared = jnp.sum(
        jnp.where(lane == FIRST + line, owner_column, 0.0)
        + jnp.where(lane == FIRST + rows + line, slot_column, 0.0),
        axis=0,
        keepdims=True,
    )
    rows_f32[:, meta_at:] = dot(packer, facts.astype(bf16)) + shared
    for d in range(dp):
        send_rows[d] = rows_f32[d * capacity : (d + 1) * capacity, :].astype(bf16)

    pl.semaphore_wait(barrier, total - 1)

    def request_copy(k):
        return pltpu.make_async_remote_copy(
            src_ref=send_rows.at[lax.rem(me + k, dp)],
            dst_ref=recv_rows.at[me],
            send_sem=send_sem.at[0, k],
            recv_sem=recv_sem.at[0, k],
            device_id=(lax.rem(me + k, dp), part),
            device_id_type=MESH,
        )

    def request_arrival(k):
        return pltpu.make_async_remote_copy(
            src_ref=send_rows.at[0],
            dst_ref=recv_rows.at[lax.rem(me + dp - k, dp)],
            send_sem=send_sem.at[0, k],
            recv_sem=recv_sem.at[0, k],
            device_id=(lax.rem(me + k, dp), part),
            device_id_type=MESH,
        )

    for k in range(1, dp):
        request_copy(k).start()
    recv_rows[me] = send_rows[me]
    slot_query[...] = jnp.zeros_like(slot_query)
    for k in range(1, dp):
        request_arrival(k).wait_recv()

    for s in range(dp):
        rows_f32[s * capacity : (s + 1) * capacity, :] = recv_rows[s].astype(f32)
    facts_in = rows_f32[:, meta_at:]
    placing_row = to_row(facts_in[:, 0:1])
    placer = jnp.where(
        placing_row == iota((slots, items), 0).astype(f32) + 1.0, 1.0, 0.0
    ).astype(bf16)
    for h in range(heads):
        g = h // GROUP
        slot_query[:, h, g * HEAD_SIZE : (g + 1) * HEAD_SIZE] = dot(
            placer, rows_f32[:, h * HEAD_SIZE : (h + 1) * HEAD_SIZE].astype(bf16)
        )
    slot_small[0] = dot(placer, rows_f32[:, query_width : query_width + kv_width].astype(bf16))
    slot_small[1] = dot(placer, rows_f32[:, query_width + kv_width : meta_at].astype(bf16))
    slot_facts = dot(placer, facts_in.astype(bf16))
    slot_task = slot_facts[:, 2:3] * 128.0 + slot_facts[:, 3:4]
    slot_small[2] = dot(
        jnp.where(slot_task == iota((slots, task_total), 1).astype(f32), 1.0, 0.0).astype(bf16),
        value_scale_ref[...],
    )
    slot_length[...] = jnp.broadcast_to(slot_facts[:, 1:2], (slots, positions))

    fetches[0].wait()
    fetches[1].wait()
    inv_root = 1.0 / math.sqrt(HEAD_SIZE)
    key_line = iota((heads, positions), 1).astype(f32)

    def attend(n, carry):
        picks = [n * TOGETHER + i for i in range(TOGETHER)]
        scores, owns, weights, own_weights, sums, tops = [], [], [], [], [], []
        for s in picks:
            scores.append(
                lax.dot_general(
                    slot_query[s].astype(bf16),
                    keys[s],
                    (((1,), (1,)), ((), ())),
                    preferred_element_type=f32,
                )
                * inv_root
            )
        for s in picks:
            owns.append(
                jnp.sum(slot_query[s] * slot_small[0, pl.ds(s, 1), :], axis=1, keepdims=True)
                * inv_root
            )
        for i, s in enumerate(picks):
            visible = key_line < slot_length[pl.ds(s, 1), :]
            shown = jnp.where(visible, scores[i], masked_score)
            tops.append(jnp.maximum(jnp.max(shown, axis=1, keepdims=True), owns[i]))
        for i, s in enumerate(picks):
            visible = key_line < slot_length[pl.ds(s, 1), :]
            shown = jnp.where(visible, scores[i], masked_score)
            weights.append(jnp.where(visible, jnp.exp(shown - tops[i]), 0.0))
            own_weights.append(jnp.exp(owns[i] - tops[i]))
        blends = [dot(weights[i].astype(bf16), values[s]) for i, s in enumerate(picks)]
        for i in range(TOGETHER):
            sums.append(jnp.sum(weights[i], axis=1, keepdims=True) + own_weights[i])
        for i, s in enumerate(picks):
            one = pl.ds(s, 1)
            blended = blends[i] + own_weights[i].astype(bf16).astype(f32) * slot_small[1, one, :]
            attended = (blended / sums[i]).astype(bf16).astype(f32) * slot_small[2, one, :]
            for g in range(kv_heads):
                slot_context[s, g * GROUP : (g + 1) * GROUP, :] = attended[
                    g * GROUP : (g + 1) * GROUP, g * HEAD_SIZE : (g + 1) * HEAD_SIZE
                ]
        return carry

    column, line_in = me // inner, lax.rem(me, inner)

    def source_of(k):
        return lax.rem(column + outer - k, outer) * inner + line_in

    def along_copy(k, c, source):
        return pltpu.make_async_remote_copy(
            src_ref=context.at[source, c],
            dst_ref=context.at[source, c],
            send_sem=along_send.at[k, c],
            recv_sem=along_recv.at[k, c],
            device_id=(lax.rem(column + k, outer) * inner + line_in, part),
            device_id_type=MESH,
        )

    def across_copy(k, j, c, source):
        return pltpu.make_async_remote_copy(
            src_ref=context.at[source, c],
            dst_ref=context.at[source, c],
            send_sem=across_send.at[k, j, c],
            recv_sem=across_recv.at[k, j, c],
            device_id=(column * inner + lax.rem(line_in + j, inner), part),
            device_id_type=MESH,
        )

    def forward(c):
        for k in (outer - 1, *range(1, outer - 1)):
            along_copy(k, c, source_of(k)).wait_recv()
            for j in range(1, inner):
                across_copy(k, j, c, source_of(k)).start()

    for c in range(chunks):
        lax.fori_loop(c * chunk // TOGETHER, (c + 1) * chunk // TOGETHER, attend, 0)
        for h in range(heads):
            context[me, c, :, h * HEAD_SIZE : (h + 1) * HEAD_SIZE] = slot_context[
                c * chunk : (c + 1) * chunk, h, :
            ].astype(bf16)
        for k in range(1, outer):
            along_copy(k, c, me).start()
        for j in range(1, inner):
            across_copy(0, j, c, me).start()
        if c > 0:
            forward(c - 1)

    lane_r = iota((rows, META), 1)
    line_r = iota((rows, META), 0)
    for s in range(dp):
        fact_row = rows_f32[s * capacity : s * capacity + 1, meta_at:]
        owner_in = jnp.sum(
            jnp.where(lane_r == FIRST + line_r, fact_row, 0.0), axis=1, keepdims=True
        )
        slot_in = jnp.sum(
            jnp.where(lane_r == FIRST + rows + line_r, fact_row, 0.0), axis=1, keepdims=True
        )
        selector[s * rows : (s + 1) * rows, :] = jnp.where(
            owner_in * slots + slot_in == iota((rows, dp * slots), 1).astype(f32), 1.0, 0.0
        ).astype(bf16)
    fetches[2].wait()
    forward(chunks - 1)
    for c in range(chunks):
        for k in range(outer):
            for j in range(1, inner):
                source = lax.rem(column + outer - k, outer) * inner + lax.rem(
                    line_in + inner - j, inner
                )
                across_copy(k, j, c, source).wait_recv()

    arranged = dot(selector[...], context[...].reshape(dp * slots, query_width)).astype(bf16)
    send_part[...] = dot(arranged, weight[...]).astype(bf16).reshape(dp, rows, columns)

    target_part = me // blocks
    place = lax.rem(me, blocks) * mp + part

    def part_copy(k):
        target = lax.rem(me + k, dp)
        return pltpu.make_async_remote_copy(
            src_ref=send_part.at[target],
            dst_ref=recv_part.at[place],
            send_sem=send_sem.at[2, k],
            recv_sem=recv_sem.at[2, place],
            device_id=(target, target_part),
            device_id_type=MESH,
        )

    def part_arrival(j):
        return pltpu.make_async_remote_copy(
            src_ref=send_part.at[0],
            dst_ref=recv_part.at[j],
            send_sem=send_sem.at[2, 0],
            recv_sem=recv_sem.at[2, j],
            device_id=(me, part),
            device_id_type=MESH,
        )

    for k in range(1, dp):
        part_copy(k).start()

    @pl.when(target_part != part)
    def _():
        part_copy(0).start()

    @pl.when(target_part == part)
    def _():
        recv_part[place] = send_part[me]

    for j in range(dp):
        own_block = (part * blocks + j // mp == me) & (part == j % mp)

        @pl.when(jnp.logical_not(own_block))
        def _():
            part_arrival(j).wait_recv()

    for e in range(blocks):
        summed = recv_part[e * mp].astype(f32)
        for j in range(1, mp):
            summed = summed + recv_part[e * mp + j].astype(f32)
        out_ref[:, e * columns : (e + 1) * columns] = summed.astype(bf16)

    for k in range(1, dp):
        request_copy(k).wait_send()
        part_copy(k).wait_send()

    for c in range(chunks):
        for k in range(outer):
            if k > 0:
                along_copy(k, c, me).wait_send()
            for j in range(1, inner):
                across_copy(k, j, c, source_of(k)).wait_send()

    @pl.when(target_part != part)
    def _():
        part_copy(0).wait_send()


def on_device(
    dp,
    mp,
    queries,
    incoming_key,
    incoming_value,
    key_cache,
    cached_values,
    task_key_scale,
    task_value_scale,
    out_weight,
    task_id,
    cached_length,
    task_owner,
    cache_slot,
):
    rows, query_width = queries.shape
    kv_width = incoming_key.shape[1]
    slots = key_cache.shape[0]
    capacity = 2 * rows // dp
    items = dp * capacity
    columns = out_weight.shape[1]
    row_width = query_width + 2 * kv_width + META
    heads = query_width // HEAD_SIZE
    outer, inner = factors(dp)
    vmem = pl.BlockSpec(memory_space=pltpu.VMEM)
    away = pl.BlockSpec(memory_space=pl.ANY)
    return pl.pallas_call(
        functools.partial(layer_kernel, dp, mp),
        out_shape=jax.ShapeDtypeStruct((rows, dp * columns // mp), bf16),
        in_specs=[vmem] * 9 + [away] * 3,
        out_specs=vmem,
        scratch_shapes=[
            pltpu.VMEM(key_cache.shape, bf16),
            pltpu.VMEM(cached_values.shape, bf16),
            pltpu.VMEM(out_weight.shape, bf16),
            pltpu.VMEM((items, row_width), f32),
            pltpu.VMEM((dp, capacity, row_width), bf16),
            pltpu.VMEM((dp, capacity, row_width), bf16),
            pltpu.VMEM((slots, heads, kv_width), f32),
            pltpu.VMEM((3, slots, kv_width), f32),
            pltpu.VMEM((slots, key_cache.shape[1]), f32),
            pltpu.VMEM((slots, heads, HEAD_SIZE), f32),
            pltpu.VMEM((dp, CHUNKS, slots // CHUNKS, query_width), bf16),
            pltpu.VMEM((dp * rows, dp * slots), bf16),
            pltpu.VMEM((dp, rows, columns), bf16),
            pltpu.VMEM((dp, rows, columns), bf16),
            pltpu.SemaphoreType.DMA((3,)),
            pltpu.SemaphoreType.DMA((3, dp)),
            pltpu.SemaphoreType.DMA((3, dp)),
            pltpu.SemaphoreType.DMA((outer, CHUNKS)),
            pltpu.SemaphoreType.DMA((outer, CHUNKS)),
            pltpu.SemaphoreType.DMA((outer, inner, CHUNKS)),
            pltpu.SemaphoreType.DMA((outer, inner, CHUNKS)),
        ],
        compiler_params=pltpu.CompilerParams(
            collective_id=0, has_side_effects=True, vmem_limit_bytes=60 * 1024 * 1024
        ),
    )(
        queries,
        incoming_key,
        incoming_value,
        task_key_scale,
        task_value_scale,
        task_id.reshape(1, -1),
        cached_length.reshape(1, -1),
        cache_slot.reshape(1, -1),
        task_owner.reshape(1, -1),
        key_cache,
        cached_values,
        out_weight,
    )


def solution(mesh):
    placed = (
        P("dp", "mp"),
        P("dp", "mp"),
        P("dp", "mp"),
        P("dp", None, "mp"),
        P("dp", None, "mp"),
        P(None, "mp"),
        P(None, "mp"),
        P("mp", "dp"),
        P("dp"),
        P("dp"),
        P(),
        P("dp"),
    )
    return jax.shard_map(
        functools.partial(on_device, mesh.shape["dp"], mesh.shape["mp"]),
        mesh=mesh,
        in_specs=placed,
        out_specs=P("dp", "mp"),
        check_vma=False,
    )
```

profile of v0, /device:TPU:1, one launch (start us, length us, event | category | flops | bytes accessed | tf_op | source)
XLA Modules:
  0.0 66.8 jit_solution(1843199554944435026)
XLA Ops:
  0.0 65.4 %shard_map.118 = bf16[16,1024]{1,0:T(8,128)(2,1)} custom-call(bf16[16,1024]{1,0:T(8,128)(2,1)} %query_ref.1, bf16[16,128]{1,0:T(8,128)(2,1)} %new_key_ref.1, bf16[16,128]{1,0:T(8,128)(2,1)} %new_value_ref.1, bf16[256,128]{1,0:T(8,128)(2,1)} %key_scale_ref.1, bf16[256,128]{1,0:T(8,128)(2,1)} %value_scale_ref.1, s32[1,16]{1,0:T(1,128)} %bitcast.5, ...), custom_call_target="tpu_custom_call" | custom-call | tf_op jit(solution)/shard_map/pallas_call | solution.py:430
  65.4 1.4 %copy.14 = bf16[16,1024]{1,0:T(8,128)(2,1)} copy(bf16[16,1024]{1,0:T(8,128)(2,1)} %shard_map.118) | data formatting | bytes 65536
where the time goes:
time: 67 us; the launch traced here: 66.8 us
  Pallas kernels  65.4 us (98%)
  local copies, waits for them, and re-layouts  1.38 us (2%)
    pallas_call x1, Pallas kernels, on_device(): pl.pallas_call(functools.partial(layer_kernel, dp, mp), out_shape=jax.Sha...  65.4 us
    unnamed x1, local copies, waits for them, and re-layouts  1.38 us

commit v1 on v0

v1 whole, which is shorter than its diff:
```python
import functools
import math

import jax
import jax.numpy as jnp
from jax import lax
from jax.experimental import pallas as pl
from jax.experimental.pallas import tpu as pltpu
from jax.sharding import PartitionSpec as P

HEAD_SIZE = 128
META = 128
TOGETHER = 8
MESH = pl.DeviceIdType.MESH

masked_score = -1e30
f32 = jnp.float32
bf16 = jnp.bfloat16


def iota(shape, dim):
    return lax.broadcasted_iota(jnp.int32, shape, dim)


def to_column(row):
    n = row.shape[1]
    eye = iota((n, n), 0) == iota((n, n), 1)
    return jnp.sum(jnp.where(eye, row, 0.0), axis=1, keepdims=True)


def to_row(column):
    n = column.shape[0]
    eye = iota((n, n), 0) == iota((n, n), 1)
    return jnp.sum(jnp.where(eye, column, 0.0), axis=0, keepdims=True)


def dot(a, b):
    return jnp.dot(a, b, preferred_element_type=f32)


def one_hot(mask):
    return jnp.where(mask, 1.0, 0.0).astype(bf16)


def layer_kernel(
    dp,
    mp,
    query_ref,
    new_key_ref,
    new_value_ref,
    key_scale_ref,
    value_scale_ref,
    task_ref,
    length_ref,
    slot_ref,
    owner_ref,
    key_hbm,
    value_hbm,
    weight_hbm,
    out_ref,
    keys,
    values,
    weights_in,
    rows_f32,
    send_rows,
    recv_rows,
    slot_query,
    slot_small,
    slot_length,
    slot_context,
    home_f32,
    home_send,
    home_recv,
    contexts,
    send_part,
    recv_part,
    local_sem,
    request_send,
    request_recv,
    home_send_sem,
    home_recv_sem,
    weight_send,
    weight_recv,
    context_send,
    context_recv,
    part_send,
    part_recv,
):
    me = lax.axis_index("dp")
    part = lax.axis_index("mp")
    rows, query_width = query_ref.shape
    kv_width = new_key_ref.shape[1]
    heads = query_width // HEAD_SIZE
    task_total = key_scale_ref.shape[0]
    slots, positions, _ = keys.shape
    columns = weights_in.shape[3]
    meta_at = query_width + 2 * kv_width
    inner = dp // mp
    outer = mp
    z, y = me // inner, lax.rem(me, inner)

    with jax.named_scope("a_greet"):
        fetches = [
            pltpu.make_async_copy(key_hbm, keys, local_sem.at[0]),
            pltpu.make_async_copy(value_hbm, values, local_sem.at[1]),
            pltpu.make_async_copy(weight_hbm, weights_in.at[y], local_sem.at[2]),
        ]
        barrier = pltpu.get_barrier_semaphore()
        for k in range(1, dp):
            pl.semaphore_signal(
                barrier, inc=1, device_id=(lax.rem(me + k, dp), part), device_id_type=MESH
            )
        for k in range(1, mp):
            pl.semaphore_signal(
                barrier, inc=1, device_id=(me, lax.rem(part + k, mp)), device_id_type=MESH
            )
        for fetch in fetches:
            fetch.start()

    with jax.named_scope("b_pack"):
        task_column = to_column(task_ref[...].astype(f32))
        length_column = to_column(length_ref[...].astype(f32))
        slot_column = to_column(slot_ref[...].astype(f32))
        picked = task_column == iota((rows, task_total), 1).astype(f32)
        owner_column = jnp.sum(
            jnp.where(picked, owner_ref[...].astype(f32), 0.0), axis=1, keepdims=True
        )
        owner_row = to_row(owner_column)
        packer = one_hot(owner_row == iota((dp, rows), 0).astype(f32))
        unpacker = one_hot(owner_column == iota((rows, dp), 1).astype(f32))
        task_rows = one_hot(picked)
        key_factor = dot(task_rows, key_scale_ref[...])
        value_factor = dot(task_rows, value_scale_ref[...])
        for h in range(heads):
            lanes = slice(h * HEAD_SIZE, (h + 1) * HEAD_SIZE)
            scaled = (query_ref[:, lanes].astype(f32) * key_factor).astype(bf16)
            rows_f32[:, lanes] = dot(packer, scaled)
        rows_f32[:, query_width : query_width + kv_width] = dot(packer, new_key_ref[...])
        rows_f32[:, query_width + kv_width : meta_at] = dot(packer, new_value_ref[...])
        lane = iota((rows, META), 1)
        facts = jnp.where(lane == 0, slot_column + 1.0, 0.0) + jnp.where(
            lane == 1, length_column, 0.0
        )
        rows_f32[:, meta_at:] = dot(packer, facts.astype(bf16))
        for d in range(dp):
            send_rows[d] = rows_f32[d : d + 1, :].astype(bf16)

    with jax.named_scope("c_barwait"):
        pl.semaphore_wait(barrier, dp + mp - 2)

    def row_copy(source, target, sends, recvs, k):
        return pltpu.make_async_remote_copy(
            src_ref=source.at[lax.rem(me + k, dp)],
            dst_ref=target.at[me],
            send_sem=sends.at[k],
            recv_sem=recvs.at[k],
            device_id=(lax.rem(me + k, dp), part),
            device_id_type=MESH,
        )

    def row_arrival(source, target, sends, recvs, k):
        return pltpu.make_async_remote_copy(
            src_ref=source.at[0],
            dst_ref=target.at[lax.rem(me + dp - k, dp)],
            send_sem=sends.at[k],
            recv_sem=recvs.at[k],
            device_id=(lax.rem(me + k, dp), part),
            device_id_type=MESH,
        )

    request = (send_rows, recv_rows, request_send, request_recv)
    homeward = (home_send, home_recv, home_send_sem, home_recv_sem)

    up = z * inner + lax.rem(y + 1, inner)
    down = z * inner + lax.rem(y + inner - 1, inner)

    def weight_copy(k, block, half, target):
        return pltpu.make_async_remote_copy(
            src_ref=weights_in.at[block, half],
            dst_ref=weights_in.at[block, half],
            send_sem=weight_send.at[k],
            recv_sem=weight_recv.at[k],
            device_id=(target, part),
            device_id_type=MESH,
        )

    y_down, y_up = lax.rem(y + inner - 1, inner), lax.rem(y + 1, inner)
    y_far = lax.rem(y + 2, inner)

    with jax.named_scope("d_reqsend"):
        for k in range(1, dp):
            row_copy(*request, k).start()
        recv_rows[me] = send_rows[me]
        fetches[2].wait()
        weight_copy(0, y, 0, up).start()
        weight_copy(1, y, 1, down).start()
        slot_query[...] = jnp.zeros_like(slot_query)
    with jax.named_scope("e_reqwait"):
        for k in range(1, dp):
            row_arrival(*request, k).wait_recv()

    with jax.named_scope("f_place"):
        for s in range(dp):
            rows_f32[s : s + 1, :] = recv_rows[s].astype(f32)
        facts_in = rows_f32[:, meta_at:]
        placing_row = to_row(facts_in[:, 0:1])
        placer = one_hot(placing_row == iota((slots, dp), 0).astype(f32) + 1.0)
        chooser = one_hot(facts_in[:, 0:1] == iota((dp, slots), 1).astype(f32) + 1.0)
        for h in range(heads):
            slot_query[:, h, :] = dot(
                placer, rows_f32[:, h * HEAD_SIZE : (h + 1) * HEAD_SIZE].astype(bf16)
            )
        slot_small[0] = dot(placer, rows_f32[:, query_width : query_width + kv_width].astype(bf16))
        slot_small[1] = dot(placer, rows_f32[:, query_width + kv_width : meta_at].astype(bf16))
        slot_facts = dot(placer, facts_in.astype(bf16))
        slot_length[...] = jnp.broadcast_to(slot_facts[:, 1:2], (slots, positions))
        fetches[0].wait()
        fetches[1].wait()

    inv_root = 1.0 / math.sqrt(HEAD_SIZE)
    key_line = iota((heads, positions), 1).astype(f32)

    def attend(n, carry):
        picks = [n * TOGETHER + i for i in range(TOGETHER)]
        scores, owns, weights, own_weights, sums, tops = [], [], [], [], [], []
        for s in picks:
            scores.append(
                lax.dot_general(
                    slot_query[s].astype(bf16),
                    keys[s],
                    (((1,), (1,)), ((), ())),
                    preferred_element_type=f32,
                )
                * inv_root
            )
        for s in picks:
            owns.append(
                jnp.sum(slot_query[s] * slot_small[0, pl.ds(s, 1), :], axis=1, keepdims=True)
                * inv_root
            )
        for i, s in enumerate(picks):
            visible = key_line < slot_length[pl.ds(s, 1), :]
            shown = jnp.where(visible, scores[i], masked_score)
            tops.append(jnp.maximum(jnp.max(shown, axis=1, keepdims=True), owns[i]))
        for i, s in enumerate(picks):
            visible = key_line < slot_length[pl.ds(s, 1), :]
            shown = jnp.where(visible, scores[i], masked_score)
            weights.append(jnp.where(visible, jnp.exp(shown - tops[i]), 0.0))
            own_weights.append(jnp.exp(owns[i] - tops[i]))
        blends = [dot(weights[i].astype(bf16), values[s]) for i, s in enumerate(picks)]
        for i in range(TOGETHER):
            sums.append(jnp.sum(weights[i], axis=1, keepdims=True) + own_weights[i])
        for i, s in enumerate(picks):
            one = pl.ds(s, 1)
            blended = blends[i] + own_weights[i].astype(bf16).astype(f32) * slot_small[1, one, :]
            slot_context[s] = blended / sums[i]
        return carry

    with jax.named_scope("g_attend"):
        lax.fori_loop(0, slots // TOGETHER, attend, 0)

    with jax.named_scope("h_choose"):
        for h in range(heads):
            home_f32[:, h * HEAD_SIZE : (h + 1) * HEAD_SIZE] = dot(
                chooser, slot_context[:, h, :].astype(bf16)
            )
        for d in range(dp):
            home_send[d] = home_f32[d : d + 1, :].astype(bf16)

    with jax.named_scope("i_homesend"):
        for k in range(1, dp):
            row_copy(*homeward, k).start()
        home_recv[me] = home_send[me]
    with jax.named_scope("j_relay"):
        weight_copy(2, y, 1, up).start()
        weight_copy(3, y, 0, down).start()
        weight_copy(0, y_down, 0, up).wait_recv()
        weight_copy(4, y_down, 0, up).start()
        weight_copy(1, y_up, 1, down).wait_recv()
        weight_copy(5, y_up, 1, down).start()
    with jax.named_scope("k_homewait"):
        for k in range(1, dp):
            row_arrival(*homeward, k).wait_recv()

    with jax.named_scope("l_compact"):
        for s in range(dp):
            home_f32[s : s + 1, :] = home_recv[s].astype(f32)
        for h in range(heads):
            lanes = slice(h * HEAD_SIZE, (h + 1) * HEAD_SIZE)
            mine = dot(unpacker, home_f32[:, lanes].astype(bf16))
            contexts[z, :, lanes] = (mine * value_factor).astype(bf16)

    def context_copy(k, block):
        return pltpu.make_async_remote_copy(
            src_ref=contexts.at[block],
            dst_ref=contexts.at[block],
            send_sem=context_send.at[k],
            recv_sem=context_recv.at[k],
            device_id=(lax.rem(z + k, outer) * inner + y, part),
            device_id_type=MESH,
        )

    with jax.named_scope("m_ctxsend"):
        for k in (4, 3, 5, 2, 6, 1, 7):
            context_copy(k, z).start()
    with jax.named_scope("n_weightwait"):
        weight_copy(2, y_down, 1, up).wait_recv()
        weight_copy(3, y_up, 0, down).wait_recv()
        weight_copy(4, y_far, 0, up).wait_recv()
        weight_copy(5, y_far, 1, down).wait_recv()
    with jax.named_scope("o_ctxwait"):
        for k in range(1, outer):
            context_copy(k, lax.rem(z + outer - k, outer)).wait_recv()

    def part_copy(n, k):
        target = lax.rem(z + k, outer)
        return pltpu.make_async_remote_copy(
            src_ref=send_part.at[n, target],
            dst_ref=recv_part.at[n, part],
            send_sem=part_send.at[n, k],
            recv_sem=part_recv.at[n, part],
            device_id=(target * inner + y, z),
            device_id_type=MESH,
        )

    def part_arrival(n, j):
        return pltpu.make_async_remote_copy(
            src_ref=send_part.at[n, 0],
            dst_ref=recv_part.at[n, j],
            send_sem=part_send.at[n, 0],
            recv_sem=part_recv.at[n, j],
            device_id=(me, part),
            device_id_type=MESH,
        )

    with jax.named_scope("p_project"):
        gathered = contexts[...].reshape(outer * rows, query_width)
        half = query_width // 2
        for n in range(inner):
            summed = dot(gathered[:, :half], weights_in[n, 0]) + dot(
                gathered[:, half:], weights_in[n, 1]
            )
            send_part[n] = summed.astype(bf16).reshape(outer, rows, columns)
            for k in (4, 3, 5, 2, 6, 1, 7):
                part_copy(n, k).start()

            @pl.when(z != part)
            def _():
                part_copy(n, 0).start()

            @pl.when(z == part)
            def _():
                recv_part[n, part] = send_part[n, z]

    with jax.named_scope("q_partwait"):
        for n in range(inner):
            for j in range(mp):

                @pl.when(jnp.logical_not((z == part) & (part == j)))
                def _():
                    part_arrival(n, j).wait_recv()

            summed = recv_part[n, 0].astype(f32)
            for j in range(1, mp):
                summed = summed + recv_part[n, j].astype(f32)
            out_ref[:, n * columns : (n + 1) * columns] = summed.astype(bf16)

    with jax.named_scope("r_drain"):
        for k in range(1, dp):
            row_copy(*request, k).wait_send()
            row_copy(*homeward, k).wait_send()
        weight_copy(0, y, 0, up).wait_send()
        weight_copy(1, y, 1, down).wait_send()
        weight_copy(2, y, 1, up).wait_send()
        weight_copy(3, y, 0, down).wait_send()
        weight_copy(4, y_down, 0, up).wait_send()
        weight_copy(5, y_up, 1, down).wait_send()
        for k in range(1, outer):
            context_copy(k, z).wait_send()
        for n in range(inner):
            for k in range(1, outer):
                part_copy(n, k).wait_send()

        @pl.when(z != part)
        def _():
            for n in range(inner):
                part_copy(n, 0).wait_send()


def on_device(
    dp,
    mp,
    queries,
    incoming_key,
    incoming_value,
    key_cache,
    cached_values,
    task_key_scale,
    task_value_scale,
    out_weight,
    task_id,
    cached_length,
    task_owner,
    cache_slot,
):
    rows, query_width = queries.shape
    kv_width = incoming_key.shape[1]
    slots = key_cache.shape[0]
    depth, columns = out_weight.shape
    row_width = query_width + 2 * kv_width + META
    heads = query_width // HEAD_SIZE
    inner = dp // mp
    vmem = pl.BlockSpec(memory_space=pltpu.VMEM)
    away = pl.BlockSpec(memory_space=pl.ANY)
    return pl.pallas_call(
        functools.partial(layer_kernel, dp, mp),
        out_shape=jax.ShapeDtypeStruct((rows, inner * columns), bf16),
        in_specs=[vmem] * 9 + [away] * 3,
        out_specs=vmem,
        scratch_shapes=[
            pltpu.VMEM(key_cache.shape, bf16),
            pltpu.VMEM(cached_values.shape, bf16),
            pltpu.VMEM((inner, 2, depth // 2, columns), bf16),
            pltpu.VMEM((dp, row_width), f32),
            pltpu.VMEM((dp, 1, row_width), bf16),
            pltpu.VMEM((dp, 1, row_width), bf16),
            pltpu.VMEM((slots, heads, kv_width), f32),
            pltpu.VMEM((2, slots, kv_width), f32),
            pltpu.VMEM((slots, key_cache.shape[1]), f32),
            pltpu.VMEM((slots, heads, HEAD_SIZE), f32),
            pltpu.VMEM((dp, query_width), f32),
            pltpu.VMEM((dp, 1, query_width), bf16),
            pltpu.VMEM((dp, 1, query_width), bf16),
            pltpu.VMEM((mp, rows, query_width), bf16),
            pltpu.VMEM((inner, mp, rows, columns), bf16),
            pltpu.VMEM((inner, mp, rows, columns), bf16),
            pltpu.SemaphoreType.DMA((3,)),
            pltpu.SemaphoreType.DMA((dp,)),
            pltpu.SemaphoreType.DMA((dp,)),
            pltpu.SemaphoreType.DMA((dp,)),
            pltpu.SemaphoreType.DMA((dp,)),
            pltpu.SemaphoreType.DMA((6,)),
            pltpu.SemaphoreType.DMA((6,)),
            pltpu.SemaphoreType.DMA((mp,)),
            pltpu.SemaphoreType.DMA((mp,)),
            pltpu.SemaphoreType.DMA((inner, mp)),
            pltpu.SemaphoreType.DMA((inner, mp)),
        ],
        compiler_params=pltpu.CompilerParams(
            collective_id=0, has_side_effects=True, vmem_limit_bytes=60 * 1024 * 1024
        ),
    )(
        queries,
        incoming_key,
        incoming_value,
        task_key_scale,
        task_value_scale,
        task_id.reshape(1, -1),
        cached_length.reshape(1, -1),
        cache_slot.reshape(1, -1),
        task_owner.reshape(1, -1),
        key_cache,
        cached_values,
        out_weight.reshape(2, depth // 2, columns),
    )


def solution(mesh):
    placed = (
        P("dp", "mp"),
        P("dp", "mp"),
        P("dp", "mp"),
        P("dp", None, "mp"),
        P("dp", None, "mp"),
        P(None, "mp"),
        P(None, "mp"),
        P("mp", "dp"),
        P("dp"),
        P("dp"),
        P(),
        P("dp"),
    )
    return jax.shard_map(
        functools.partial(on_device, mesh.shape["dp"], mesh.shape["mp"]),
        mesh=mesh,
        in_specs=placed,
        out_specs=P("dp", "mp"),
        check_vma=False,
    )
```

time: 67 us -> 48.2 us (0.72)
  Pallas kernels: 65.4 us -> 46.6 us
    pallas_call x1, Pallas kernels: 65.4 us -> 46.6 us  [on_device(): pl.pallas_call(functools.partial(layer_kernel, dp, mp), out_shape=jax.Sha...]
where the time goes in v1:
time: 48.2 us; the launch traced here: 48 us
  Pallas kernels  46.6 us (97%)
  local copies, waits for them, and re-layouts  1.38 us (3%)
    pallas_call x1, Pallas kernels, on_device(): pl.pallas_call(functools.partial(layer_kernel, dp, mp), out_shape=jax.Sha...  46.6 us
    unnamed x1, local copies, waits for them, and re-layouts  1.38 us

profile of v1, /device:TPU:1, one launch (start us, length us, event | category | flops | bytes accessed | tf_op | source)
XLA Modules:
  0.0 48.0 jit_solution(3892986446420718977)
XLA Ops:
  0.0 46.6 %shard_map.118 = bf16[16,1024]{1,0:T(8,128)(2,1)} custom-call(bf16[16,1024]{1,0:T(8,128)(2,1)} %query_ref.1, bf16[16,128]{1,0:T(8,128)(2,1)} %new_key_ref.1, bf16[16,128]{1,0:T(8,128)(2,1)} %new_value_ref.1, bf16[256,128]{1,0:T(8,128)(2,1)} %key_scale_ref.1, bf16[256,128]{1,0:T(8,128)(2,1)} %value_scale_ref.1, s32[1,16]{1,0:T(1,128)} %bitcast.7, ...), custom_call_target="tpu_custom_call" | custom-call | tf_op jit(solution)/shard_map/pallas_call | solution.py:415
  46.6 1.4 %copy.14 = bf16[16,1024]{1,0:T(8,128)(2,1)} copy(bf16[16,1024]{1,0:T(8,128)(2,1)} %shard_map.118) | data formatting | bytes 65536

commit v2 on v1

v2 whole, which is shorter than its diff:
```python
import functools
import math

import jax
import jax.numpy as jnp
from jax import lax
from jax.experimental import pallas as pl
from jax.experimental.pallas import tpu as pltpu
from jax.sharding import PartitionSpec as P

HEAD_SIZE = 128
PAGE = 16
TOGETHER = 8
MESH = pl.DeviceIdType.MESH

masked_score = -1e30
f32 = jnp.float32
bf16 = jnp.bfloat16


def iota(shape, dim):
    return lax.broadcasted_iota(jnp.int32, shape, dim)


def ring(k, n):
    return min(k, n - k)


def to_column(row):
    n = row.shape[1]
    eye = iota((n, n), 0) == iota((n, n), 1)
    return jnp.sum(jnp.where(eye, row, 0.0), axis=1, keepdims=True)


def to_row(column):
    n = column.shape[0]
    eye = iota((n, n), 0) == iota((n, n), 1)
    return jnp.sum(jnp.where(eye, column, 0.0), axis=0, keepdims=True)


def dot(a, b):
    return jnp.dot(a, b, preferred_element_type=f32)


def one_hot(mask):
    return jnp.where(mask, 1.0, 0.0).astype(bf16)


def layer_kernel(
    dp,
    mp,
    query_hbm,
    new_key_hbm,
    new_value_hbm,
    key_scale_hbm,
    value_scale_hbm,
    task_hbm,
    length_hbm,
    slot_hbm,
    owner_hbm,
    key_hbm,
    value_hbm,
    weight_hbm,
    out_ref,
    query_ref,
    new_key_ref,
    new_value_ref,
    key_scale_ref,
    value_scale_ref,
    task_ref,
    length_ref,
    slot_ref,
    owner_ref,
    keys,
    values,
    weights_in,
    weights_over,
    send_rows,
    recv_rows,
    home_send,
    home_recv,
    selector,
    factor,
    contexts,
    block,
    send_part,
    recv_part,
    local_sem,
    small_sem,
    request_send,
    request_recv,
    home_send_sem,
    home_recv_sem,
    weight_send,
    weight_recv,
    over_send,
    over_recv,
    context_send,
    context_recv,
    part_send,
    part_recv,
):
    me = lax.axis_index("dp")
    part = lax.axis_index("mp")
    rows, query_width = query_ref.shape
    heads = query_width // HEAD_SIZE
    task_total = key_scale_ref.shape[0]
    slots, positions, _ = keys.shape
    columns = weights_in.shape[3]
    inner = dp // mp
    outer = mp
    z, y = me // inner, lax.rem(me, inner)
    chip, core = part // 2, lax.rem(part, 2)
    other = 2 * chip + 1 - core

    def at(kz, ky):
        return lax.rem(z + kz, outer) * inner + lax.rem(y + ky, inner)

    def distance(offset):
        return ring(offset[0], outer) + ring(offset[1], inner)

    def back(offset):
        return (outer - offset[0]) % outer, (inner - offset[1]) % inner

    near = sorted(((kz, ky) for kz in range(outer) for ky in range(inner)), key=distance)
    far = near[:0:-1]

    with jax.named_scope("a_greet"):
        small = [
            pltpu.make_async_copy(away, here, small_sem.at[i])
            for i, (away, here) in enumerate(
                (
                    (task_hbm, task_ref),
                    (owner_hbm, owner_ref),
                    (slot_hbm, slot_ref),
                    (length_hbm, length_ref),
                    (query_hbm, query_ref),
                    (key_scale_hbm, key_scale_ref),
                    (value_scale_hbm, value_scale_ref),
                    (new_key_hbm, new_key_ref),
                    (new_value_hbm, new_value_ref),
                )
            )
        ]
        for copy in small:
            copy.start()
        barrier = pltpu.get_barrier_semaphore()
        for kz, ky in far:
            pl.semaphore_signal(
                barrier, inc=1, device_id=(at(kz, ky), part), device_id_type=MESH
            )
        for k in range(1, mp):
            pl.semaphore_signal(
                barrier, inc=1, device_id=(me, lax.rem(part + k, mp)), device_id_type=MESH
            )
        fetches = [
            pltpu.make_async_copy(weight_hbm, weights_in.at[y], local_sem.at[2]),
            pltpu.make_async_copy(key_hbm, keys, local_sem.at[0]),
            pltpu.make_async_copy(value_hbm, values, local_sem.at[1]),
        ]
        for fetch in fetches:
            fetch.start()
        for copy in small:
            copy.wait()

    with jax.named_scope("b_pack"):
        task_column = to_column(task_ref[...].astype(f32))
        length_column = to_column(length_ref[...].astype(f32))
        slot_column = to_column(slot_ref[...].astype(f32))
        picked = task_column == iota((rows, task_total), 1).astype(f32)
        owner_column = jnp.sum(
            jnp.where(picked, owner_ref[...].astype(f32), 0.0), axis=1, keepdims=True
        )
        owner_row = to_row(owner_column)
        task_rows = one_hot(picked)
        key_factor = dot(task_rows, key_scale_ref[...])
        factor[...] = dot(task_rows, value_scale_ref[...])
        pieces = []
        for h in range(heads):
            lanes = slice(h * HEAD_SIZE, (h + 1) * HEAD_SIZE)
            pieces.append((query_ref[:, lanes].astype(f32) * key_factor).astype(bf16))
        pieces.append(new_key_ref[...])
        pieces.append(new_value_ref[...])
        pieces.append(jnp.broadcast_to(slot_column, (rows, HEAD_SIZE)).astype(bf16))
        pieces.append(jnp.broadcast_to(length_column, (rows, HEAD_SIZE)).astype(bf16))
        wide = len(pieces) * rows
        spread = one_hot(lax.rem(iota((rows, wide), 1), rows) == iota((rows, wide), 0))
        owner_wide = dot(owner_row.astype(bf16), spread)
        line = iota((dp * PAGE, wide), 0)
        lane = iota((dp * PAGE, wide), 1)
        packer = one_hot(
            (lax.rem(line, PAGE) == lane // rows) & ((line // PAGE).astype(f32) == owner_wide)
        )
        packed = dot(packer, jnp.concatenate(pieces, axis=0))
        send_rows[...] = packed.astype(bf16).reshape(dp, PAGE, HEAD_SIZE)
        line = iota((heads * rows, dp * heads), 0)
        lane = iota((heads * rows, dp * heads), 1)
        same = lax.rem(iota((heads * rows, rows), 0), rows) == iota((heads * rows, rows), 1)
        owner_tall = jnp.sum(jnp.where(same, owner_row, 0.0), axis=1, keepdims=True)
        selector[...] = one_hot(
            (line // rows == lax.rem(lane, heads)) & ((lane // heads).astype(f32) == owner_tall)
        )

    with jax.named_scope("c_barwait"):
        pl.semaphore_wait(barrier, dp + mp - 2)

    def row_copy(source, target, sends, recvs, offset, slot):
        k = offset[0] * inner + offset[1]
        return pltpu.make_async_remote_copy(
            src_ref=source.at[at(*offset)],
            dst_ref=target.at[slot],
            send_sem=sends.at[k],
            recv_sem=recvs.at[k],
            device_id=(at(*offset), part),
            device_id_type=MESH,
        )

    request = (send_rows, recv_rows, request_send, request_recv)
    homeward = (home_send, home_recv, home_send_sem, home_recv_sem)

    up, down = at(0, 1), at(0, inner - 1)
    y_up, y_down, y_far = (lax.rem(y + k, inner) for k in (1, inner - 1, 2))

    def weight_copy(k, source, half, target):
        return pltpu.make_async_remote_copy(
            src_ref=weights_in.at[source, half],
            dst_ref=weights_in.at[source, half],
            send_sem=weight_send.at[k],
            recv_sem=weight_recv.at[k],
            device_id=(target, part),
            device_id_type=MESH,
        )

    def over_copy(k, source, half):
        return pltpu.make_async_remote_copy(
            src_ref=weights_in.at[source, half],
            dst_ref=weights_over.at[source, half],
            send_sem=over_send.at[k, half],
            recv_sem=over_recv.at[k, half],
            device_id=(me, other),
            device_id_type=MESH,
        )

    with jax.named_scope("d_reqsend"):
        for offset in far:
            row_copy(*request, offset, me).start()
        recv_rows[me] = send_rows[me]
        fetches[0].wait()
        weight_copy(0, y, 0, up).start()
        weight_copy(1, y, 1, down).start()
        over_copy(0, y, 0).start()
        over_copy(0, y, 1).start()
        fetches[1].wait()
        fetches[2].wait()

    inv_root = 1.0 / math.sqrt(HEAD_SIZE)
    key_line = lax.rem(iota((heads, positions), 1), HEAD_SIZE).astype(f32)

    def attend(sources):
        queries, extras, picks, limits = [], [], [], []
        for s in sources:
            page = recv_rows[s]
            queries.append(page[:heads])
            extra = page[heads:].astype(f32)
            extras.append(extra)
            picks.append(jnp.clip(jnp.max(extra[2:3]).astype(jnp.int32), 0, slots - 1))
            length = jnp.broadcast_to(extra[3:4], (heads, HEAD_SIZE))
            limits.append(
                jnp.concatenate(
                    [length - i * HEAD_SIZE for i in range(positions // HEAD_SIZE)], axis=1
                )
            )
        scores = [
            lax.dot_general(
                q, keys[p], (((1,), (1,)), ((), ())), preferred_element_type=f32
            )
            * inv_root
            for q, p in zip(queries, picks)
        ]
        owns = [
            jnp.sum(q.astype(f32) * extra[0:1], axis=1, keepdims=True) * inv_root
            for q, extra in zip(queries, extras)
        ]
        shown = [
            jnp.where(key_line < limit, score, masked_score)
            for score, limit in zip(scores, limits)
        ]
        tops = [
            jnp.maximum(jnp.max(score, axis=1, keepdims=True), own)
            for score, own in zip(shown, owns)
        ]
        weights = [
            jnp.where(key_line < limit, jnp.exp(score - top), 0.0)
            for score, limit, top in zip(shown, limits, tops)
        ]
        own_weights = [jnp.exp(own - top) for own, top in zip(owns, tops)]
        blends = [dot(weight.astype(bf16), values[p]) for weight, p in zip(weights, picks)]
        sums = [
            jnp.sum(weight, axis=1, keepdims=True) + own
            for weight, own in zip(weights, own_weights)
        ]
        for s, blend, own, extra, total in zip(sources, blends, own_weights, extras, sums):
            blended = blend + own.astype(bf16).astype(f32) * extra[1:2]
            home_send[s] = (blended / total).astype(bf16)

    for g in range(0, dp, TOGETHER):
        group = near[g : g + TOGETHER]
        with jax.named_scope("e_reqwait"):
            for offset in group:
                if offset != (0, 0):
                    row_copy(*request, offset, at(*back(offset))).wait_recv()
        with jax.named_scope("f_attend"):
            attend([at(*back(offset)) for offset in group])
        with jax.named_scope("g_homesend"):
            for offset in reversed(group):
                if offset != (0, 0):
                    row_copy(*homeward, back(offset), me).start()
            if g == 0:
                home_recv[me] = home_send[me]

    with jax.named_scope("j_relay"):
        weight_copy(2, y, 1, up).start()
        weight_copy(3, y, 0, down).start()
        weight_copy(0, y_down, 0, up).wait_recv()
        weight_copy(4, y_down, 0, up).start()
        over_copy(1, y_down, 0).start()
        weight_copy(1, y_up, 1, down).wait_recv()
        weight_copy(5, y_up, 1, down).start()
        over_copy(2, y_up, 1).start()
    with jax.named_scope("k_homewait"):
        for offset in near[1:]:
            row_copy(*homeward, offset, at(*back(offset))).wait_recv()

    mine = lax.rem(z, 2)

    with jax.named_scope("l_compact"):
        chosen = dot(selector[...], home_recv[...].reshape(dp * heads, HEAD_SIZE))
        for h in range(heads):
            block[:, h * HEAD_SIZE : (h + 1) * HEAD_SIZE] = (
                chosen[h * rows : (h + 1) * rows] * factor[...]
            ).astype(bf16)

    def context_copy(k, home):
        return pltpu.make_async_remote_copy(
            src_ref=block,
            dst_ref=contexts.at[core, home],
            send_sem=context_send.at[k],
            recv_sem=context_recv.at[core, home],
            device_id=(at(k, 0), 2 * chip + mine),
            device_id_type=MESH,
        )

    def context_arrival(source, home):
        return pltpu.make_async_remote_copy(
            src_ref=block,
            dst_ref=contexts.at[source, home],
            send_sem=context_send.at[0],
            recv_sem=context_recv.at[source, home],
            device_id=(me, other),
            device_id_type=MESH,
        )

    with jax.named_scope("m_ctxsend"):
        for k in (4, 3, 5, 2, 6, 1, 7):
            context_copy(k, z // 2).start()

        @pl.when(mine != core)
        def _():
            context_copy(0, z // 2).start()

        @pl.when(mine == core)
        def _():
            contexts[core, z // 2] = block[...]

    with jax.named_scope("n_overs"):
        weight_copy(2, y_down, 1, up).wait_recv()
        over_copy(1, y_down, 1).start()
        weight_copy(3, y_up, 0, down).wait_recv()
        over_copy(2, y_up, 0).start()
        weight_copy(4, y_far, 0, up).wait_recv()
        over_copy(3, y_far, 0).start()
        weight_copy(5, y_far, 1, down).wait_recv()
        over_copy(3, y_far, 1).start()
    with jax.named_scope("o_ctxwait"):
        for source in range(2):
            for home in range(outer // 2):

                @pl.when(jnp.logical_not((source == core) & (2 * home + core == z)))
                def _():
                    context_arrival(source, home).wait_recv()

    with jax.named_scope("o_overwait"):
        for half in range(2):
            over_copy(0, y, half).wait_recv()
            over_copy(1, y_down, half).wait_recv()
            over_copy(2, y_up, half).wait_recv()
            over_copy(3, y_far, half).wait_recv()

    shift = lax.rem(z + core, 2)

    def part_copy(n, i):
        target = lax.rem(z + 2 * i + shift, outer)
        return pltpu.make_async_remote_copy(
            src_ref=send_part.at[n, target // 2],
            dst_ref=recv_part.at[n, chip],
            send_sem=part_send.at[n, i],
            recv_sem=part_recv.at[n, chip],
            device_id=(target * inner + y, z),
            device_id_type=MESH,
        )

    def part_arrival(n, j):
        return pltpu.make_async_remote_copy(
            src_ref=send_part.at[n, 0],
            dst_ref=recv_part.at[n, j],
            send_sem=part_send.at[n, 0],
            recv_sem=part_recv.at[n, j],
            device_id=(me, other),
            device_id_type=MESH,
        )

    with jax.named_scope("p_project"):
        half = query_width // 2
        direct = contexts[core].reshape(outer * rows // 2, query_width)
        over = contexts[1 - core].reshape(outer * rows // 2, query_width)
        for n in range(inner):
            summed = (
                dot(direct[:, :half], weights_in[n, 0])
                + dot(direct[:, half:], weights_in[n, 1])
                + dot(over[:, :half], weights_over[n, 0])
                + dot(over[:, half:], weights_over[n, 1])
            )
            send_part[n] = summed.astype(bf16).reshape(outer // 2, rows, columns)
            for i in (2, 1, 3):
                part_copy(n, i).start()

            @pl.when(z != part)
            def _():
                part_copy(n, 0).start()

            @pl.when(z == part)
            def _():
                recv_part[n, chip] = send_part[n, z // 2]

    with jax.named_scope("q_drain"):
        for offset in far:
            row_copy(*request, offset, me).wait_send()
            row_copy(*homeward, offset, me).wait_send()
        weight_copy(0, y, 0, up).wait_send()
        weight_copy(1, y, 1, down).wait_send()
        weight_copy(2, y, 1, up).wait_send()
        weight_copy(3, y, 0, down).wait_send()
        weight_copy(4, y_down, 0, up).wait_send()
        weight_copy(5, y_up, 1, down).wait_send()
        for half in range(2):
            for k in range(inner):
                over_copy(k, y, half).wait_send()
        for k in range(1, outer):
            context_copy(k, z // 2).wait_send()

        @pl.when(mine != core)
        def _():
            context_copy(0, z // 2).wait_send()

    with jax.named_scope("r_partwait"):
        for n in range(inner):
            for j in range(mp // 2):

                @pl.when(jnp.logical_not((z == part) & (chip == j)))
                def _():
                    part_arrival(n, j).wait_recv()

            summed = recv_part[n, 0].astype(f32)
            for j in range(1, mp // 2):
                summed = summed + recv_part[n, j].astype(f32)
            out_ref[:, n * columns : (n + 1) * columns] = summed.astype(bf16)

    with jax.named_scope("s_drain"):
        for n in range(inner):
            for i in range(1, mp // 2):
                part_copy(n, i).wait_send()

        @pl.when(z != part)
        def _():
            for n in range(inner):
                part_copy(n, 0).wait_send()


def on_device(
    dp,
    mp,
    queries,
    incoming_key,
    incoming_value,
    key_cache,
    cached_values,
    task_key_scale,
    task_value_scale,
    out_weight,
    task_id,
    cached_length,
    task_owner,
    cache_slot,
):
    rows, query_width = queries.shape
    depth, columns = out_weight.shape
    heads = query_width // HEAD_SIZE
    inner = dp // mp
    small = (
        queries,
        incoming_key,
        incoming_value,
        task_key_scale,
        task_value_scale,
        task_id.reshape(1, -1),
        cached_length.reshape(1, -1),
        cache_slot.reshape(1, -1),
        task_owner.reshape(1, -1),
    )
    away = pl.BlockSpec(memory_space=pl.ANY)
    return pl.pallas_call(
        functools.partial(layer_kernel, dp, mp),
        out_shape=jax.ShapeDtypeStruct((rows, inner * columns), bf16),
        in_specs=[away] * 12,
        out_specs=pl.BlockSpec(memory_space=pltpu.VMEM),
        scratch_shapes=[pltpu.VMEM(array.shape, array.dtype) for array in small]
        + [
            pltpu.VMEM(key_cache.shape, bf16),
            pltpu.VMEM(cached_values.shape, bf16),
            pltpu.VMEM((inner, 2, depth // 2, columns), bf16),
            pltpu.VMEM((inner, 2, depth // 2, columns), bf16),
            pltpu.VMEM((dp, PAGE, HEAD_SIZE), bf16),
            pltpu.VMEM((dp, PAGE, HEAD_SIZE), bf16),
            pltpu.VMEM((dp, heads, HEAD_SIZE), bf16),
            pltpu.VMEM((dp, heads, HEAD_SIZE), bf16),
            pltpu.VMEM((heads * rows, dp * heads), bf16),
            pltpu.VMEM((rows, HEAD_SIZE), f32),
            pltpu.VMEM((2, mp // 2, rows, query_width), bf16),
            pltpu.VMEM((rows, query_width), bf16),
            pltpu.VMEM((inner, mp // 2, rows, columns), bf16),
            pltpu.VMEM((inner, mp // 2, rows, columns), bf16),
            pltpu.SemaphoreType.DMA((3,)),
            pltpu.SemaphoreType.DMA((len(small),)),
            pltpu.SemaphoreType.DMA((dp,)),
            pltpu.SemaphoreType.DMA((dp,)),
            pltpu.SemaphoreType.DMA((dp,)),
            pltpu.SemaphoreType.DMA((dp,)),
            pltpu.SemaphoreType.DMA((6,)),
            pltpu.SemaphoreType.DMA((6,)),
            pltpu.SemaphoreType.DMA((inner, 2)),
            pltpu.SemaphoreType.DMA((inner, 2)),
            pltpu.SemaphoreType.DMA((mp,)),
            pltpu.SemaphoreType.DMA((2, mp // 2)),
            pltpu.SemaphoreType.DMA((inner, mp // 2)),
            pltpu.SemaphoreType.DMA((inner, mp // 2)),
        ],
        compiler_params=pltpu.CompilerParams(
            collective_id=0, has_side_effects=True, vmem_limit_bytes=60 * 1024 * 1024
        ),
    )(*small, key_cache, cached_values, out_weight.reshape(2, depth // 2, columns))


def solution(mesh):
    placed = (
        P("dp", "mp"),
        P("dp", "mp"),
        P("dp", "mp"),
        P("dp", None, "mp"),
        P("dp", None, "mp"),
        P(None, "mp"),
        P(None, "mp"),
        P("mp", "dp"),
        P("dp"),
        P("dp"),
        P(),
        P("dp"),
    )
    return jax.shard_map(
        functools.partial(on_device, mesh.shape["dp"], mesh.shape["mp"]),
        mesh=mesh,
        in_specs=placed,
        out_specs=P("dp", "mp"),
        check_vma=False,
    )
```

time: 48.2 us -> 43.8 us (0.909)
  Pallas kernels: 46.6 us -> 42.3 us
    pallas_call x1, Pallas kernels: 46.6 us -> 42.3 us  [on_device(): pl.pallas_call(functools.partial(layer_kernel, dp, mp), out_shape=jax.Sha...]
where the time goes in v2:
time: 43.8 us; the launch traced here: 43.7 us
  Pallas kernels  42.3 us (97%)
  local copies, waits for them, and re-layouts  1.38 us (3%)
    pallas_call x1, Pallas kernels, on_device(): pl.pallas_call(functools.partial(layer_kernel, dp, mp), out_shape=jax.Sha...  42.3 us
    unnamed x1, local copies, waits for them, and re-layouts  1.38 us

profile of v2, /device:TPU:1, one launch (start us, length us, event | category | flops | bytes accessed | tf_op | source)
XLA Modules:
  0.0 43.7 jit_solution(17636634221342795421)
XLA Ops:
  0.0 42.3 %shard_map.118 = bf16[16,1024]{1,0:T(8,128)(2,1)} custom-call(bf16[16,1024]{1,0:T(8,128)(2,1)} %query_hbm.1, bf16[16,128]{1,0:T(8,128)(2,1)} %new_key_hbm.1, bf16[16,128]{1,0:T(8,128)(2,1)} %new_value_hbm.1, bf16[256,128]{1,0:T(8,128)(2,1)} %key_scale_hbm.1, bf16[256,128]{1,0:T(8,128)(2,1)} %value_scale_hbm.1, s32[1,16]{1,0:T(1,128)} %bitcast.7, ...), custom_call_target="tpu_custom_call" | custom-call | tf_op jit(solution)/shard_map/pallas_call | solution.py:521
  42.3 1.4 %copy.14 = bf16[16,1024]{1,0:T(8,128)(2,1)} copy(bf16[16,1024]{1,0:T(8,128)(2,1)} %shard_map.118) | data formatting | bytes 65536

commit v3 on v2

--- a/solution.py
+++ b/solution.py
@@ -87,17 +87,12 @@
     recv_part,
     local_sem,
     small_sem,
-    request_send,
+    send_sem,
     request_recv,
-    home_send_sem,
     home_recv_sem,
-    weight_send,
     weight_recv,
-    over_send,
     over_recv,
-    context_send,
     context_recv,
-    part_send,
     part_recv,
 ):
     me = lax.axis_index("dp")
@@ -124,6 +119,7 @@
 
     near = sorted(((kz, ky) for kz in range(outer) for ky in range(inner)), key=distance)
     far = near[:0:-1]
+    group_of = {offset: n // TOGETHER for n, offset in enumerate(near)}
 
     with jax.named_scope("a_greet"):
         small = [
@@ -204,46 +200,87 @@
     with jax.named_scope("c_barwait"):
         pl.semaphore_wait(barrier, dp + mp - 2)
 
-    def row_copy(source, target, sends, recvs, offset, slot):
-        k = offset[0] * inner + offset[1]
+    def remote(source, target, send_sem, recv_sem, device):
         return pltpu.make_async_remote_copy(
-            src_ref=source.at[at(*offset)],
-            dst_ref=target.at[slot],
-            send_sem=sends.at[k],
-            recv_sem=recvs.at[k],
-            device_id=(at(*offset), part),
+            src_ref=source,
+            dst_ref=target,
+            send_sem=send_sem,
+            recv_sem=recv_sem,
+            device_id=device,
             device_id_type=MESH,
         )
 
-    request = (send_rows, recv_rows, request_send, request_recv)
-    homeward = (home_send, home_recv, home_send_sem, home_recv_sem)
+    def request_copy(offset):
+        return remote(
+            send_rows.at[at(*offset)],
+            recv_rows.at[me],
+            send_sem.at[0],
+            request_recv.at[group_of[offset]],
+            (at(*offset), part),
+        )
+
+    def requests_in(group, count):
+        pages = pl.ds(0, count)
+        return remote(
+            send_rows.at[pages],
+            recv_rows.at[pages],
+            send_sem.at[0],
+            request_recv.at[group],
+            (me, other),
+        )
+
+    def home_copy(offset):
+        return remote(
+            home_send.at[at(*offset)],
+            home_recv.at[me],
+            send_sem.at[1],
+            home_recv_sem.at[0],
+            (at(*offset), part),
+        )
+
+    def homes_in():
+        pages = pl.ds(0, dp - 1)
+        return remote(
+            home_send.at[pages],
+            home_recv.at[pages],
+            send_sem.at[1],
+            home_recv_sem.at[0],
+            (me, other),
+        )
 
     up, down = at(0, 1), at(0, inner - 1)
     y_up, y_down, y_far = (lax.rem(y + k, inner) for k in (1, inner - 1, 2))
 
     def weight_copy(k, source, half, target):
-        return pltpu.make_async_remote_copy(
-            src_ref=weights_in.at[source, half],
-            dst_ref=weights_in.at[source, half],
-            send_sem=weight_send.at[k],
-            recv_sem=weight_recv.at[k],
-            device_id=(target, part),
-            device_id_type=MESH,
+        return remote(
+            weights_in.at[source, half],
+            weights_in.at[source, half],
+            send_sem.at[2],
+            weight_recv.at[k],
+            (target, part),
         )
 
     def over_copy(k, source, half):
-        return pltpu.make_async_remote_copy(
-            src_ref=weights_in.at[source, half],
-            dst_ref=weights_over.at[source, half],
-            send_sem=over_send.at[k, half],
-            recv_sem=over_recv.at[k, half],
-            device_id=(me, other),
-            device_id_type=MESH,
+        return remote(
+            weights_in.at[source, half],
+            weights_over.at[source, half],
+            send_sem.at[3],
+            over_recv.at[k],
+            (me, other),
+        )
+
+    def over_in(k, source):
+        return remote(
+            weights_in.at[source],
+            weights_over.at[source],
+            send_sem.at[3],
+            over_recv.at[k],
+            (me, other),
         )
 
     with jax.named_scope("d_reqsend"):
         for offset in far:
-            row_copy(*request, offset, me).start()
+            request_copy(offset).start()
         recv_rows[me] = send_rows[me]
         fetches[0].wait()
         weight_copy(0, y, 0, up).start()
@@ -306,15 +343,13 @@
     for g in range(0, dp, TOGETHER):
         group = near[g : g + TOGETHER]
         with jax.named_scope("e_reqwait"):
-            for offset in group:
-                if offset != (0, 0):
-                    row_copy(*request, offset, at(*back(offset))).wait_recv()
+            requests_in(g // TOGETHER, TOGETHER if g > 0 else TOGETHER - 1).wait_recv()
         with jax.named_scope("f_attend"):
             attend([at(*back(offset)) for offset in group])
         with jax.named_scope("g_homesend"):
             for offset in reversed(group):
                 if offset != (0, 0):
-                    row_copy(*homeward, back(offset), me).start()
+                    home_copy(back(offset)).start()
             if g == 0:
                 home_recv[me] = home_send[me]
 
@@ -328,8 +363,7 @@
         weight_copy(5, y_up, 1, down).start()
         over_copy(2, y_up, 1).start()
     with jax.named_scope("k_homewait"):
-        for offset in near[1:]:
-            row_copy(*homeward, offset, at(*back(offset))).wait_recv()
+        homes_in().wait_recv()
 
     mine = lax.rem(z, 2)
 
@@ -340,150 +374,163 @@
                 chosen[h * rows : (h + 1) * rows] * factor[...]
             ).astype(bf16)
 
-    def context_copy(k, home):
-        return pltpu.make_async_remote_copy(
-            src_ref=block,
-            dst_ref=contexts.at[core, home],
-            send_sem=context_send.at[k],
-            recv_sem=context_recv.at[core, home],
-            device_id=(at(k, 0), 2 * chip + mine),
-            device_id_type=MESH,
-        )
-
-    def context_arrival(source, home):
-        return pltpu.make_async_remote_copy(
-            src_ref=block,
-            dst_ref=contexts.at[source, home],
-            send_sem=context_send.at[0],
-            recv_sem=context_recv.at[source, home],
-            device_id=(me, other),
-            device_id_type=MESH,
-        )
+    homes = outer // 2
+    middle = query_width // 2
+
+    def place(source, home):
+        return source * homes + lax.rem(home, outer) // 2
+
+    def context_copy(k):
+        return remote(
+            block,
+            contexts.at[place(core, z)],
+            send_sem.at[4],
+            context_recv.at[{2: 1, 6: 2}.get(k, 0)],
+            (at(k, 0), 2 * chip + mine),
+        )
+
+    def context_relay(source, k, half):
+        spot = contexts.at[place(source, z + outer - k), :, pl.ds(half * middle, middle)]
+        return remote(spot, spot, send_sem.at[4], context_recv.at[0], (at(k, 0), part))
+
+    def contexts_in(k, count):
+        blocks = contexts.at[pl.ds(0, count)]
+        return remote(blocks, blocks, send_sem.at[4], context_recv.at[k], (me, other))
 
     with jax.named_scope("m_ctxsend"):
-        for k in (4, 3, 5, 2, 6, 1, 7):
-            context_copy(k, z // 2).start()
+        for k in (2, 6, 3, 5, 1, 7):
+            context_copy(k).start()
 
         @pl.when(mine != core)
         def _():
-            context_copy(0, z // 2).start()
+            context_copy(0).start()
 
         @pl.when(mine == core)
         def _():
-            contexts[core, z // 2] = block[...]
+            contexts[place(core, z)] = block[...]
 
     with jax.named_scope("n_overs"):
         weight_copy(2, y_down, 1, up).wait_recv()
         over_copy(1, y_down, 1).start()
         weight_copy(3, y_up, 0, down).wait_recv()
         over_copy(2, y_up, 0).start()
+
+    with jax.named_scope("n_relay"):
+
+        @pl.when(mine == core)
+        def _():
+            contexts_in(1, 2).wait_recv()
+            for source in range(2):
+                context_relay(source, 2, 0).start()
+            contexts_in(2, 2).wait_recv()
+            for source in range(2):
+                context_relay(source, outer - 2, 1).start()
+
+    with jax.named_scope("n_overs2"):
         weight_copy(4, y_far, 0, up).wait_recv()
         over_copy(3, y_far, 0).start()
         weight_copy(5, y_far, 1, down).wait_recv()
         over_copy(3, y_far, 1).start()
+
     with jax.named_scope("o_ctxwait"):
-        for source in range(2):
-            for home in range(outer // 2):
-
-                @pl.when(jnp.logical_not((source == core) & (2 * home + core == z)))
-                def _():
-                    context_arrival(source, home).wait_recv()
-
-    with jax.named_scope("o_overwait"):
-        for half in range(2):
-            over_copy(0, y, half).wait_recv()
-            over_copy(1, y_down, half).wait_recv()
-            over_copy(2, y_up, half).wait_recv()
-            over_copy(3, y_far, half).wait_recv()
+
+        @pl.when(mine == core)
+        def _():
+            contexts_in(0, 3).wait_recv()
+
+        @pl.when(mine != core)
+        def _():
+            contexts_in(0, 2 * homes).wait_recv()
 
     shift = lax.rem(z + core, 2)
 
-    def part_copy(n, i):
+    def part_copy(n, column, i):
         target = lax.rem(z + 2 * i + shift, outer)
-        return pltpu.make_async_remote_copy(
-            src_ref=send_part.at[n, target // 2],
-            dst_ref=recv_part.at[n, chip],
-            send_sem=part_send.at[n, i],
-            recv_sem=part_recv.at[n, chip],
-            device_id=(target * inner + y, z),
-            device_id_type=MESH,
-        )
-
-    def part_arrival(n, j):
-        return pltpu.make_async_remote_copy(
-            src_ref=send_part.at[n, 0],
-            dst_ref=recv_part.at[n, j],
-            send_sem=part_send.at[n, 0],
-            recv_sem=part_recv.at[n, j],
-            device_id=(me, other),
-            device_id_type=MESH,
-        )
+        return remote(
+            send_part.at[column, target // 2],
+            recv_part.at[column, chip],
+            send_sem.at[5],
+            part_recv.at[n],
+            (target * inner + y, z),
+        )
+
+    def parts_in(n, count):
+        parts = pl.ds(0, count)
+        return remote(
+            send_part.at[0, parts],
+            recv_part.at[0, parts],
+            send_sem.at[5],
+            part_recv.at[n],
+            (me, other),
+        )
+
+    order = (y, y_down, y_up, y_far)
 
     with jax.named_scope("p_project"):
-        half = query_width // 2
-        direct = contexts[core].reshape(outer * rows // 2, query_width)
-        over = contexts[1 - core].reshape(outer * rows // 2, query_width)
-        for n in range(inner):
+        direct = contexts[pl.ds(core * homes, homes)].reshape(homes * rows, query_width)
+        over = contexts[pl.ds((1 - core) * homes, homes)].reshape(homes * rows, query_width)
+        for n, column in enumerate(order):
+            over_in(n, column).wait_recv()
             summed = (
-                dot(direct[:, :half], weights_in[n, 0])
-                + dot(direct[:, half:], weights_in[n, 1])
-                + dot(over[:, :half], weights_over[n, 0])
-                + dot(over[:, half:], weights_over[n, 1])
+                dot(direct[:, :middle], weights_in[column, 0])
+                + dot(direct[:, middle:], weights_in[column, 1])
+                + dot(over[:, :middle], weights_over[column, 0])
+                + dot(over[:, middle:], weights_over[column, 1])
             )
-            send_part[n] = summed.astype(bf16).reshape(outer // 2, rows, columns)
+            send_part[column] = summed.astype(bf16).reshape(homes, rows, columns)
             for i in (2, 1, 3):
-                part_copy(n, i).start()
+                part_copy(n, column, i).start()
 
             @pl.when(z != part)
             def _():
-                part_copy(n, 0).start()
+                part_copy(n, column, 0).start()
 
             @pl.when(z == part)
             def _():
-                recv_part[n, chip] = send_part[n, z // 2]
+                recv_part[column, chip] = send_part[column, z // 2]
 
     with jax.named_scope("q_drain"):
-        for offset in far:
-            row_copy(*request, offset, me).wait_send()
-            row_copy(*homeward, offset, me).wait_send()
-        weight_copy(0, y, 0, up).wait_send()
-        weight_copy(1, y, 1, down).wait_send()
-        weight_copy(2, y, 1, up).wait_send()
-        weight_copy(3, y, 0, down).wait_send()
-        weight_copy(4, y_down, 0, up).wait_send()
-        weight_copy(5, y_up, 1, down).wait_send()
-        for half in range(2):
-            for k in range(inner):
-                over_copy(k, y, half).wait_send()
-        for k in range(1, outer):
-            context_copy(k, z // 2).wait_send()
+        requests_in(0, dp - 1).wait_send()
+        homes_in().wait_send()
+        three = weights_in.at[pl.ds(0, inner - 1)]
+        remote(three, three, send_sem.at[2], weight_recv.at[0], (me, other)).wait_send()
+        remote(weights_in, weights_over, send_sem.at[3], over_recv.at[0], (me, other)).wait_send()
+
+        @pl.when(mine == core)
+        def _():
+            contexts_in(0, 2 * homes).wait_send()
 
         @pl.when(mine != core)
         def _():
-            context_copy(0, z // 2).wait_send()
+            contexts_in(0, 2 * homes - 1).wait_send()
 
     with jax.named_scope("r_partwait"):
-        for n in range(inner):
-            for j in range(mp // 2):
-
-                @pl.when(jnp.logical_not((z == part) & (chip == j)))
-                def _():
-                    part_arrival(n, j).wait_recv()
-
-            summed = recv_part[n, 0].astype(f32)
+        for n, column in enumerate(order):
+
+            @pl.when(z != part)
+            def _():
+                parts_in(n, mp // 2).wait_recv()
+
+            @pl.when(z == part)
+            def _():
+                parts_in(n, mp // 2 - 1).wait_recv()
+
+            summed = recv_part[column, 0].astype(f32)
             for j in range(1, mp // 2):
-                summed = summed + recv_part[n, j].astype(f32)
-            out_ref[:, n * columns : (n + 1) * columns] = summed.astype(bf16)
+                summed = summed + recv_part[column, j].astype(f32)
+            start = pl.multiple_of(column * columns, columns)
+            out_ref[:, pl.ds(start, columns)] = summed.astype(bf16)
 
     with jax.named_scope("s_drain"):
-        for n in range(inner):
-            for i in range(1, mp // 2):
-                part_copy(n, i).wait_send()
 
         @pl.when(z != part)
         def _():
-            for n in range(inner):
-                part_copy(n, 0).wait_send()
+            remote(send_part, send_part, send_sem.at[5], part_recv.at[0], (me, other)).wait_send()
+
+        @pl.when(z == part)
+        def _():
+            most = send_part.at[:, pl.ds(0, mp // 2 - 1)]
+            remote(most, most, send_sem.at[5], part_recv.at[0], (me, other)).wait_send()
 
 
 def on_device(
@@ -535,24 +582,19 @@
             pltpu.VMEM((dp, heads, HEAD_SIZE), bf16),
             pltpu.VMEM((heads * rows, dp * heads), bf16),
             pltpu.VMEM((rows, HEAD_SIZE), f32),
-            pltpu.VMEM((2, mp // 2, rows, query_width), bf16),
+            pltpu.VMEM((mp, rows, query_width), bf16),
             pltpu.VMEM((rows, query_width), bf16),
             pltpu.VMEM((inner, mp // 2, rows, columns), bf16),
             pltpu.VMEM((inner, mp // 2, rows, columns), bf16),
             pltpu.SemaphoreType.DMA((3,)),
             pltpu.SemaphoreType.DMA((len(small),)),
-            pltpu.SemaphoreType.DMA((dp,)),
-            pltpu.SemaphoreType.DMA((dp,)),
-            pltpu.SemaphoreType.DMA((dp,)),
-            pltpu.SemaphoreType.DMA((dp,)),
             pltpu.SemaphoreType.DMA((6,)),
+            pltpu.SemaphoreType.DMA((dp // TOGETHER,)),
+            pltpu.SemaphoreType.DMA((1,)),
             pltpu.SemaphoreType.DMA((6,)),
-            pltpu.SemaphoreType.DMA((inner, 2)),
-            pltpu.SemaphoreType.DMA((inner, 2)),
-            pltpu.SemaphoreType.DMA((mp,)),
-            pltpu.SemaphoreType.DMA((2, mp // 2)),
-            pltpu.SemaphoreType.DMA((inner, mp // 2)),
-            pltpu.SemaphoreType.DMA((inner, mp // 2)),
+            pltpu.SemaphoreType.DMA((inner,)),
+            pltpu.SemaphoreType.DMA((3,)),
+            pltpu.SemaphoreType.DMA((inner,)),
         ],
         compiler_params=pltpu.CompilerParams(
             collective_id=0, has_side_effects=True, vmem_limit_bytes=60 * 1024 * 1024

time: 43.8 us -> 41.9 us (0.957)
  Pallas kernels: 42.3 us -> 40.3 us
    pallas_call x1, Pallas kernels: 42.3 us -> 40.3 us  [on_device(): pl.pallas_call(functools.partial(layer_kernel, dp, mp), out_shape=jax.Sha...]
where the time goes in v3:
time: 41.9 us; the launch traced here: 41.7 us
  Pallas kernels  40.3 us (96%)
  local copies, waits for them, and re-layouts  1.38 us (3%)
    pallas_call x1, Pallas kernels, on_device(): pl.pallas_call(functools.partial(layer_kernel, dp, mp), out_shape=jax.Sha...  40.3 us
    unnamed x1, local copies, waits for them, and re-layouts  1.38 us

profile of v3, /device:TPU:1, one launch (start us, length us, event | category | flops | bytes accessed | tf_op | source)
XLA Modules:
  0.0 41.7 jit_solution(7290624904646852971)
XLA Ops:
  0.0 40.3 %shard_map.118 = bf16[16,1024]{1,0:T(8,128)(2,1)} custom-call(bf16[16,1024]{1,0:T(8,128)(2,1)} %query_hbm.1, bf16[16,128]{1,0:T(8,128)(2,1)} %new_key_hbm.1, bf16[16,128]{1,0:T(8,128)(2,1)} %new_value_hbm.1, bf16[256,128]{1,0:T(8,128)(2,1)} %key_scale_hbm.1, bf16[256,128]{1,0:T(8,128)(2,1)} %value_scale_hbm.1, s32[1,16]{1,0:T(1,128)} %bitcast.7, ...), custom_call_target="tpu_custom_call" | custom-call | tf_op jit(solution)/shard_map/pallas_call | solution.py:568
  40.3 1.4 %copy.14 = bf16[16,1024]{1,0:T(8,128)(2,1)} copy(bf16[16,1024]{1,0:T(8,128)(2,1)} %shard_map.118) | data formatting | bytes 65536

commit v4 on v3

--- a/solution.py
+++ b/solution.py
@@ -10,7 +10,8 @@
 
 HEAD_SIZE = 128
 PAGE = 16
-TOGETHER = 8
+TOGETHER = 32
+QUARTERS = 4
 MESH = pl.DeviceIdType.MESH
 
 masked_score = -1e30
@@ -121,6 +122,48 @@
     far = near[:0:-1]
     group_of = {offset: n // TOGETHER for n, offset in enumerate(near)}
 
+    def remote(source, target, send_sem, recv_sem, device):
+        return pltpu.make_async_remote_copy(
+            src_ref=source,
+            dst_ref=target,
+            send_sem=send_sem,
+            recv_sem=recv_sem,
+            device_id=device,
+            device_id_type=MESH,
+        )
+
+    def signal(sem, device):
+        pl.semaphore_signal(sem, inc=1, device_id=device, device_id_type=MESH)
+
+    up, down = at(0, 1), at(0, inner - 1)
+    y_up, y_down, y_far = (lax.rem(y + k, inner) for k in (1, inner - 1, 2))
+
+    def up_copy(source, q, relay):
+        piece = weights_in.at[source, q]
+        return remote(piece, piece, send_sem.at[2], weight_recv.at[relay, 0, q], (up, part))
+
+    def down_copy(source, q, relay):
+        piece = weights_in.at[source, q]
+        return remote(piece, piece, send_sem.at[2], weight_recv.at[relay, 1, q], (down, part))
+
+    def over_copy(k, source, q):
+        return remote(
+            weights_in.at[source, q],
+            weights_over.at[source, q],
+            send_sem.at[3],
+            over_recv.at[k],
+            (me, other),
+        )
+
+    def over_in(k, source):
+        return remote(
+            weights_in.at[source],
+            weights_over.at[source],
+            send_sem.at[3],
+            over_recv.at[k],
+            (me, other),
+        )
+
     with jax.named_scope("a_greet"):
         small = [
             pltpu.make_async_copy(away, here, small_sem.at[i])
@@ -142,13 +185,9 @@
             copy.start()
         barrier = pltpu.get_barrier_semaphore()
         for kz, ky in far:
-            pl.semaphore_signal(
-                barrier, inc=1, device_id=(at(kz, ky), part), device_id_type=MESH
-            )
+            signal(barrier, (at(kz, ky), part))
         for k in range(1, mp):
-            pl.semaphore_signal(
-                barrier, inc=1, device_id=(me, lax.rem(part + k, mp)), device_id_type=MESH
-            )
+            signal(barrier, (me, lax.rem(part + k, mp)))
         fetches = [
             pltpu.make_async_copy(weight_hbm, weights_in.at[y], local_sem.at[2]),
             pltpu.make_async_copy(key_hbm, keys, local_sem.at[0]),
@@ -156,6 +195,7 @@
         ]
         for fetch in fetches:
             fetch.start()
+    with jax.named_scope("a_first"):
         for copy in small:
             copy.wait()
 
@@ -197,19 +237,6 @@
             (line // rows == lax.rem(lane, heads)) & ((lane // heads).astype(f32) == owner_tall)
         )
 
-    with jax.named_scope("c_barwait"):
-        pl.semaphore_wait(barrier, dp + mp - 2)
-
-    def remote(source, target, send_sem, recv_sem, device):
-        return pltpu.make_async_remote_copy(
-            src_ref=source,
-            dst_ref=target,
-            send_sem=send_sem,
-            recv_sem=recv_sem,
-            device_id=device,
-            device_id_type=MESH,
-        )
-
     def request_copy(offset):
         return remote(
             send_rows.at[at(*offset)],
@@ -248,45 +275,21 @@
             (me, other),
         )
 
-    up, down = at(0, 1), at(0, inner - 1)
-    y_up, y_down, y_far = (lax.rem(y + k, inner) for k in (1, inner - 1, 2))
-
-    def weight_copy(k, source, half, target):
-        return remote(
-            weights_in.at[source, half],
-            weights_in.at[source, half],
-            send_sem.at[2],
-            weight_recv.at[k],
-            (target, part),
-        )
-
-    def over_copy(k, source, half):
-        return remote(
-            weights_in.at[source, half],
-            weights_over.at[source, half],
-            send_sem.at[3],
-            over_recv.at[k],
-            (me, other),
-        )
-
-    def over_in(k, source):
-        return remote(
-            weights_in.at[source],
-            weights_over.at[source],
-            send_sem.at[3],
-            over_recv.at[k],
-            (me, other),
-        )
-
+    with jax.named_scope("c_barwait"):
+        pl.semaphore_wait(barrier, dp + mp - 2)
     with jax.named_scope("d_reqsend"):
         for offset in far:
             request_copy(offset).start()
         recv_rows[me] = send_rows[me]
         fetches[0].wait()
-        weight_copy(0, y, 0, up).start()
-        weight_copy(1, y, 1, down).start()
-        over_copy(0, y, 0).start()
-        over_copy(0, y, 1).start()
+        up_copy(y, 0, 0).start()
+        down_copy(y, 2, 0).start()
+        up_copy(y, 1, 0).start()
+        down_copy(y, 3, 0).start()
+        up_copy(y, 2, 0).start()
+        down_copy(y, 0, 0).start()
+        for q in range(QUARTERS):
+            over_copy(0, y, q).start()
         fetches[1].wait()
         fetches[2].wait()
 
@@ -354,14 +357,15 @@
                 home_recv[me] = home_send[me]
 
     with jax.named_scope("j_relay"):
-        weight_copy(2, y, 1, up).start()
-        weight_copy(3, y, 0, down).start()
-        weight_copy(0, y_down, 0, up).wait_recv()
-        weight_copy(4, y_down, 0, up).start()
-        over_copy(1, y_down, 0).start()
-        weight_copy(1, y_up, 1, down).wait_recv()
-        weight_copy(5, y_up, 1, down).start()
-        over_copy(2, y_up, 1).start()
+        up_copy(y, 3, 0).start()
+        down_copy(y, 1, 0).start()
+        for q in (0, 1):
+            up_copy(y_down, q, 0).wait_recv()
+            up_copy(y_down, q, 1).start()
+            over_copy(1, y_down, q).start()
+            down_copy(y_up, q + 2, 0).wait_recv()
+            down_copy(y_up, q + 2, 1).start()
+            over_copy(2, y_up, q + 2).start()
     with jax.named_scope("k_homewait"):
         homes_in().wait_recv()
 
@@ -376,6 +380,7 @@
 
     homes = outer // 2
     middle = query_width // 2
+    quarter = query_width // QUARTERS
 
     def place(source, home):
         return source * homes + lax.rem(home, outer) // 2
@@ -385,7 +390,7 @@
             block,
             contexts.at[place(core, z)],
             send_sem.at[4],
-            context_recv.at[{2: 1, 6: 2}.get(k, 0)],
+            context_recv.at[0],
             (at(k, 0), 2 * chip + mine),
         )
 
@@ -398,7 +403,7 @@
         return remote(blocks, blocks, send_sem.at[4], context_recv.at[k], (me, other))
 
     with jax.named_scope("m_ctxsend"):
-        for k in (2, 6, 3, 5, 1, 7):
+        for k in (4, 3, 5, 2, 6, 1, 7):
             context_copy(k).start()
 
         @pl.when(mine != core)
@@ -410,33 +415,24 @@
             contexts[place(core, z)] = block[...]
 
     with jax.named_scope("n_overs"):
-        weight_copy(2, y_down, 1, up).wait_recv()
-        over_copy(1, y_down, 1).start()
-        weight_copy(3, y_up, 0, down).wait_recv()
-        over_copy(2, y_up, 0).start()
-
-    with jax.named_scope("n_relay"):
+        for q in (0, 1):
+            up_copy(y_down, q + 2, 0).wait_recv()
+            over_copy(1, y_down, q + 2).start()
+            down_copy(y_up, q, 0).wait_recv()
+            over_copy(2, y_up, q).start()
+
+    with jax.named_scope("n_overs2"):
+        for q in (0, 1):
+            up_copy(y_far, q, 1).wait_recv()
+            over_copy(3, y_far, q).start()
+            down_copy(y_far, q + 2, 1).wait_recv()
+            over_copy(3, y_far, q + 2).start()
+
+    with jax.named_scope("o_ctxwait"):
 
         @pl.when(mine == core)
         def _():
-            contexts_in(1, 2).wait_recv()
-            for source in range(2):
-                context_relay(source, 2, 0).start()
-            contexts_in(2, 2).wait_recv()
-            for source in range(2):
-                context_relay(source, outer - 2, 1).start()
-
-    with jax.named_scope("n_overs2"):
-        weight_copy(4, y_far, 0, up).wait_recv()
-        over_copy(3, y_far, 0).start()
-        weight_copy(5, y_far, 1, down).wait_recv()
-        over_copy(3, y_far, 1).start()
-
-    with jax.named_scope("o_ctxwait"):
-
-        @pl.when(mine == core)
-        def _():
-            contexts_in(0, 3).wait_recv()
+            contexts_in(0, 7).wait_recv()
 
         @pl.when(mine != core)
         def _():
@@ -471,12 +467,11 @@
         over = contexts[pl.ds((1 - core) * homes, homes)].reshape(homes * rows, query_width)
         for n, column in enumerate(order):
             over_in(n, column).wait_recv()
-            summed = (
-                dot(direct[:, :middle], weights_in[column, 0])
-                + dot(direct[:, middle:], weights_in[column, 1])
-                + dot(over[:, :middle], weights_over[column, 0])
-                + dot(over[:, middle:], weights_over[column, 1])
-            )
+            summed = jnp.zeros((homes * rows, columns), f32)
+            for q in range(QUARTERS):
+                depth = slice(q * quarter, (q + 1) * quarter)
+                summed = summed + dot(direct[:, depth], weights_in[column, q])
+                summed = summed + dot(over[:, depth], weights_over[column, q])
             send_part[column] = summed.astype(bf16).reshape(homes, rows, columns)
             for i in (2, 1, 3):
                 part_copy(n, column, i).start()
@@ -493,16 +488,16 @@
         requests_in(0, dp - 1).wait_send()
         homes_in().wait_send()
         three = weights_in.at[pl.ds(0, inner - 1)]
-        remote(three, three, send_sem.at[2], weight_recv.at[0], (me, other)).wait_send()
+        remote(three, three, send_sem.at[2], weight_recv.at[0, 0, 0], (me, other)).wait_send()
         remote(weights_in, weights_over, send_sem.at[3], over_recv.at[0], (me, other)).wait_send()
 
         @pl.when(mine == core)
         def _():
+            contexts_in(0, 2 * homes - 1).wait_send()
+
+        @pl.when(mine != core)
+        def _():
             contexts_in(0, 2 * homes).wait_send()
-
-        @pl.when(mine != core)
-        def _():
-            contexts_in(0, 2 * homes - 1).wait_send()
 
     with jax.named_scope("r_partwait"):
         for n, column in enumerate(order):
@@ -574,8 +569,8 @@
         + [
             pltpu.VMEM(key_cache.shape, bf16),
             pltpu.VMEM(cached_values.shape, bf16),
-            pltpu.VMEM((inner, 2, depth // 2, columns), bf16),
-            pltpu.VMEM((inner, 2, depth // 2, columns), bf16),
+            pltpu.VMEM((inner, QUARTERS, depth // QUARTERS, columns), bf16),
+            pltpu.VMEM((inner, QUARTERS, depth // QUARTERS, columns), bf16),
             pltpu.VMEM((dp, PAGE, HEAD_SIZE), bf16),
             pltpu.VMEM((dp, PAGE, HEAD_SIZE), bf16),
             pltpu.VMEM((dp, heads, HEAD_SIZE), bf16),
@@ -591,7 +586,7 @@
             pltpu.SemaphoreType.DMA((6,)),
             pltpu.SemaphoreType.DMA((dp // TOGETHER,)),
             pltpu.SemaphoreType.DMA((1,)),
-            pltpu.SemaphoreType.DMA((6,)),
+            pltpu.SemaphoreType.DMA((2, 2, QUARTERS)),
             pltpu.SemaphoreType.DMA((inner,)),
             pltpu.SemaphoreType.DMA((3,)),
             pltpu.SemaphoreType.DMA((inner,)),
@@ -599,7 +594,7 @@
         compiler_params=pltpu.CompilerParams(
             collective_id=0, has_side_effects=True, vmem_limit_bytes=60 * 1024 * 1024
         ),
-    )(*small, key_cache, cached_values, out_weight.reshape(2, depth // 2, columns))
+    )(*small, key_cache, cached_values, out_weight.reshape(QUARTERS, depth // QUARTERS, columns))
 
 
 def solution(mesh):

time: 41.9 us -> 41 us (0.979)
  Pallas kernels: 40.3 us -> 39.4 us
    pallas_call x1, Pallas kernels: 40.3 us -> 39.4 us  [on_device(): pl.pallas_call(functools.partial(layer_kernel, dp, mp), out_shape=jax.Sha...]
where the time goes in v4:
time: 41 us; the launch traced here: 40.8 us
  Pallas kernels  39.4 us (96%)
  local copies, waits for them, and re-layouts  1.38 us (3%)
    pallas_call x1, Pallas kernels, on_device(): pl.pallas_call(functools.partial(layer_kernel, dp, mp), out_shape=jax.Sha...  39.4 us
    unnamed x1, local copies, waits for them, and re-layouts  1.38 us

profile of v4, /device:TPU:1, one launch (start us, length us, event | category | flops | bytes accessed | tf_op | source)
XLA Modules:
  0.0 40.8 jit_solution(7143411216966490046)
XLA Ops:
  0.0 39.4 %shard_map.118 = bf16[16,1024]{1,0:T(8,128)(2,1)} custom-call(bf16[16,1024]{1,0:T(8,128)(2,1)} %query_hbm.1, bf16[16,128]{1,0:T(8,128)(2,1)} %new_key_hbm.1, bf16[16,128]{1,0:T(8,128)(2,1)} %new_value_hbm.1, bf16[256,128]{1,0:T(8,128)(2,1)} %key_scale_hbm.1, bf16[256,128]{1,0:T(8,128)(2,1)} %value_scale_hbm.1, s32[1,16]{1,0:T(1,128)} %bitcast.7, ...), custom_call_target="tpu_custom_call" | custom-call | tf_op jit(solution)/shard_map/pallas_call | solution.py:563
  39.4 1.4 %copy.14 = bf16[16,1024]{1,0:T(8,128)(2,1)} copy(bf16[16,1024]{1,0:T(8,128)(2,1)} %shard_map.118) | data formatting | bytes 65536

commit v5 on v4

--- a/solution.py
+++ b/solution.py
@@ -559,7 +559,7 @@
         cache_slot.reshape(1, -1),
         task_owner.reshape(1, -1),
     )
-    away = pl.BlockSpec(memory_space=pl.ANY)
+    away = pl.BlockSpec(memory_space=pltpu.HBM)
     return pl.pallas_call(
         functools.partial(layer_kernel, dp, mp),
         out_shape=jax.ShapeDtypeStruct((rows, inner * columns), bf16),
@@ -592,9 +592,19 @@
             pltpu.SemaphoreType.DMA((inner,)),
         ],
         compiler_params=pltpu.CompilerParams(
-            collective_id=0, has_side_effects=True, vmem_limit_bytes=60 * 1024 * 1024
+            collective_id=0, has_side_effects=True, vmem_limit_bytes=20 * 1024 * 1024
         ),
-    )(*small, key_cache, cached_values, out_weight.reshape(QUARTERS, depth // QUARTERS, columns))
+    )(
+        *[
+            pltpu.with_memory_space_constraint(array, pltpu.HBM)
+            for array in (
+                *small,
+                key_cache,
+                cached_values,
+                out_weight.reshape(QUARTERS, depth // QUARTERS, columns),
+            )
+        ]
+    )
 
 
 def solution(mesh):

time: 41 us -> 39.6 us (0.966)
  local copies, waits for them, and re-layouts: 1.38 us -> 0.62 us
  Pallas kernels: 39.4 us -> 38.9 us
    unnamed x1, local copies, waits for them, and re-layouts: 1.38 us -> 0.62 us
    pallas_call x1, Pallas kernels: 39.4 us -> 38.9 us  [on_device(): pl.pallas_call(functools.partial(layer_kernel, dp, mp), out_shape=jax.Sha...]
where the time goes in v5:
time: 39.6 us; the launch traced here: 39.5 us
  Pallas kernels  38.9 us (98%)
  local copies, waits for them, and re-layouts  0.62 us (2%)
    pallas_call x1, Pallas kernels, on_device(): pl.pallas_call(functools.partial(layer_kernel, dp, mp), out_shape=jax.Sha...  38.9 us

profile of v5, /device:TPU:1, one launch (start us, length us, event | category | flops | bytes accessed | tf_op | source)
XLA Modules:
  0.0 39.5 jit_solution(1312426209844274338)
XLA Ops:
  0.0 38.9 %shard_map.118 = bf16[16,1024]{1,0:T(8,128)(2,1)S(1)} custom-call(bf16[16,1024]{1,0:T(8,128)(2,1)} %query_hbm.1, bf16[16,128]{1,0:T(8,128)(2,1)} %new_key_hbm.1, bf16[16,128]{1,0:T(8,128)(2,1)} %new_value_hbm.1, bf16[256,128]{1,0:T(8,128)(2,1)} %key_scale_hbm.1, bf16[256,128]{1,0:T(8,128)(2,1)} %value_scale_hbm.1, s32[1,16]{1,0:T(1,128)} %bitcast.7, ...), custom_call_target="tpu_custom_call" | custom-call | tf_op jit(solution)/shard_map/pallas_call | solution.py:563
  38.9 0.6 %copy.14 = bf16[16,1024]{1,0:T(8,128)(2,1)} copy(bf16[16,1024]{1,0:T(8,128)(2,1)S(1)} %shard_map.118) | data formatting | bytes 65536

commit v6 on v5

--- a/solution.py
+++ b/solution.py
@@ -9,8 +9,7 @@
 from jax.sharding import PartitionSpec as P
 
 HEAD_SIZE = 128
-PAGE = 16
-TOGETHER = 32
+EXTRA = 4
 QUARTERS = 4
 MESH = pl.DeviceIdType.MESH
 
@@ -77,7 +76,9 @@
     weights_in,
     weights_over,
     send_rows,
+    send_extra,
     recv_rows,
+    recv_extra,
     home_send,
     home_recv,
     selector,
@@ -120,7 +121,6 @@
 
     near = sorted(((kz, ky) for kz in range(outer) for ky in range(inner)), key=distance)
     far = near[:0:-1]
-    group_of = {offset: n // TOGETHER for n, offset in enumerate(near)}
 
     def remote(source, target, send_sem, recv_sem, device):
         return pltpu.make_async_remote_copy(
@@ -222,13 +222,15 @@
         wide = len(pieces) * rows
         spread = one_hot(lax.rem(iota((rows, wide), 1), rows) == iota((rows, wide), 0))
         owner_wide = dot(owner_row.astype(bf16), spread)
-        line = iota((dp * PAGE, wide), 0)
-        lane = iota((dp * PAGE, wide), 1)
-        packer = one_hot(
-            (lax.rem(line, PAGE) == lane // rows) & ((line // PAGE).astype(f32) == owner_wide)
-        )
-        packed = dot(packer, jnp.concatenate(pieces, axis=0))
-        send_rows[...] = packed.astype(bf16).reshape(dp, PAGE, HEAD_SIZE)
+        ready_rows = jnp.concatenate(pieces, axis=0)
+        for into, first, count in ((send_rows, 0, heads), (send_extra, heads, EXTRA)):
+            line = iota((dp * count, wide), 0)
+            lane = iota((dp * count, wide), 1)
+            packer = one_hot(
+                (lax.rem(line, count) + first == lane // rows)
+                & ((line // count).astype(f32) == owner_wide)
+            )
+            into[...] = dot(packer, ready_rows).astype(bf16).reshape(dp, count, HEAD_SIZE)
         line = iota((heads * rows, dp * heads), 0)
         lane = iota((heads * rows, dp * heads), 1)
         same = lax.rem(iota((heads * rows, rows), 0), rows) == iota((heads * rows, rows), 1)
@@ -238,23 +240,33 @@
         )
 
     def request_copy(offset):
-        return remote(
-            send_rows.at[at(*offset)],
-            recv_rows.at[me],
-            send_sem.at[0],
-            request_recv.at[group_of[offset]],
-            (at(*offset), part),
-        )
-
-    def requests_in(group, count):
-        pages = pl.ds(0, count)
-        return remote(
-            send_rows.at[pages],
-            recv_rows.at[pages],
-            send_sem.at[0],
-            request_recv.at[group],
-            (me, other),
-        )
+        return [
+            remote(
+                source.at[at(*offset)],
+                target.at[me],
+                send_sem.at[sem],
+                request_recv.at[n],
+                (at(*offset), part),
+            )
+            for n, (source, target, sem) in enumerate(
+                ((send_rows, recv_rows, 0), (send_extra, recv_extra, 6))
+            )
+        ]
+
+    def requests_in():
+        pages = pl.ds(0, dp - 1)
+        return [
+            remote(
+                source.at[pages],
+                target.at[pages],
+                send_sem.at[sem],
+                request_recv.at[n],
+                (me, other),
+            )
+            for n, (source, target, sem) in enumerate(
+                ((send_rows, recv_rows, 0), (send_extra, recv_extra, 6))
+            )
+        ]
 
     def home_copy(offset):
         return remote(
@@ -279,8 +291,10 @@
         pl.semaphore_wait(barrier, dp + mp - 2)
     with jax.named_scope("d_reqsend"):
         for offset in far:
-            request_copy(offset).start()
+            for copy in request_copy(offset):
+                copy.start()
         recv_rows[me] = send_rows[me]
+        recv_extra[me] = send_extra[me]
         fetches[0].wait()
         up_copy(y, 0, 0).start()
         down_copy(y, 2, 0).start()
@@ -299,9 +313,8 @@
     def attend(sources):
         queries, extras, picks, limits = [], [], [], []
         for s in sources:
-            page = recv_rows[s]
-            queries.append(page[:heads])
-            extra = page[heads:].astype(f32)
+            queries.append(recv_rows[s])
+            extra = recv_extra[s].astype(f32)
             extras.append(extra)
             picks.append(jnp.clip(jnp.max(extra[2:3]).astype(jnp.int32), 0, slots - 1))
             length = jnp.broadcast_to(extra[3:4], (heads, HEAD_SIZE))
@@ -343,18 +356,15 @@
             blended = blend + own.astype(bf16).astype(f32) * extra[1:2]
             home_send[s] = (blended / total).astype(bf16)
 
-    for g in range(0, dp, TOGETHER):
-        group = near[g : g + TOGETHER]
-        with jax.named_scope("e_reqwait"):
-            requests_in(g // TOGETHER, TOGETHER if g > 0 else TOGETHER - 1).wait_recv()
-        with jax.named_scope("f_attend"):
-            attend([at(*back(offset)) for offset in group])
-        with jax.named_scope("g_homesend"):
-            for offset in reversed(group):
-                if offset != (0, 0):
-                    home_copy(back(offset)).start()
-            if g == 0:
-                home_recv[me] = home_send[me]
+    with jax.named_scope("e_reqwait"):
+        for copy in requests_in():
+            copy.wait_recv()
+    with jax.named_scope("f_attend"):
+        attend([at(*back(offset)) for offset in near])
+    with jax.named_scope("g_homesend"):
+        for offset in reversed(near[1:]):
+            home_copy(back(offset)).start()
+        home_recv[me] = home_send[me]
 
     with jax.named_scope("j_relay"):
         up_copy(y, 3, 0).start()
@@ -421,13 +431,6 @@
             down_copy(y_up, q, 0).wait_recv()
             over_copy(2, y_up, q).start()
 
-    with jax.named_scope("n_overs2"):
-        for q in (0, 1):
-            up_copy(y_far, q, 1).wait_recv()
-            over_copy(3, y_far, q).start()
-            down_copy(y_far, q + 2, 1).wait_recv()
-            over_copy(3, y_far, q + 2).start()
-
     with jax.named_scope("o_ctxwait"):
 
         @pl.when(mine == core)
@@ -466,6 +469,12 @@
         direct = contexts[pl.ds(core * homes, homes)].reshape(homes * rows, query_width)
         over = contexts[pl.ds((1 - core) * homes, homes)].reshape(homes * rows, query_width)
         for n, column in enumerate(order):
+            if n == 3:
+                for m in (0, 1):
+                    up_copy(y_far, m, 1).wait_recv()
+                    over_copy(3, y_far, m).start()
+                    down_copy(y_far, m + 2, 1).wait_recv()
+                    over_copy(3, y_far, m + 2).start()
             over_in(n, column).wait_recv()
             summed = jnp.zeros((homes * rows, columns), f32)
             for q in range(QUARTERS):
@@ -485,7 +494,8 @@
                 recv_part[column, chip] = send_part[column, z // 2]
 
     with jax.named_scope("q_drain"):
-        requests_in(0, dp - 1).wait_send()
+        for copy in requests_in():
+            copy.wait_send()
         homes_in().wait_send()
         three = weights_in.at[pl.ds(0, inner - 1)]
         remote(three, three, send_sem.at[2], weight_recv.at[0, 0, 0], (me, other)).wait_send()
@@ -571,8 +581,10 @@
             pltpu.VMEM(cached_values.shape, bf16),
             pltpu.VMEM((inner, QUARTERS, depth // QUARTERS, columns), bf16),
             pltpu.VMEM((inner, QUARTERS, depth // QUARTERS, columns), bf16),
-            pltpu.VMEM((dp, PAGE, HEAD_SIZE), bf16),
-            pltpu.VMEM((dp, PAGE, HEAD_SIZE), bf16),
+            pltpu.VMEM((dp, heads, HEAD_SIZE), bf16),
+            pltpu.VMEM((dp, EXTRA, HEAD_SIZE), bf16),
+            pltpu.VMEM((dp, heads, HEAD_SIZE), bf16),
+            pltpu.VMEM((dp, EXTRA, HEAD_SIZE), bf16),
             pltpu.VMEM((dp, heads, HEAD_SIZE), bf16),
             pltpu.VMEM((dp, heads, HEAD_SIZE), bf16),
             pltpu.VMEM((heads * rows, dp * heads), bf16),
@@ -583,8 +595,8 @@
             pltpu.VMEM((inner, mp // 2, rows, columns), bf16),
             pltpu.SemaphoreType.DMA((3,)),
             pltpu.SemaphoreType.DMA((len(small),)),
-            pltpu.SemaphoreType.DMA((6,)),
-            pltpu.SemaphoreType.DMA((dp // TOGETHER,)),
+            pltpu.SemaphoreType.DMA((7,)),
+            pltpu.SemaphoreType.DMA((2,)),
             pltpu.SemaphoreType.DMA((1,)),
             pltpu.SemaphoreType.DMA((2, 2, QUARTERS)),
             pltpu.SemaphoreType.DMA((inner,)),

time: 39.6 us -> 38.9 us (0.982)
  Pallas kernels: 38.9 us -> 38.2 us
    pallas_call x1, Pallas kernels: 38.9 us -> 38.2 us  [on_device(): pl.pallas_call(functools.partial(layer_kernel, dp, mp), out_shape=jax.Sha...]
where the time goes in v6:
time: 38.9 us; the launch traced here: 38.8 us
  Pallas kernels  38.2 us (98%)
  local copies, waits for them, and re-layouts  0.62 us (2%)
    pallas_call x1, Pallas kernels, on_device(): pl.pallas_call(functools.partial(layer_kernel, dp, mp), out_shape=jax.Sha...  38.2 us

profile of v6, /device:TPU:1, one launch (start us, length us, event | category | flops | bytes accessed | tf_op | source)
XLA Modules:
  0.0 38.8 jit_solution(11302335021143588915)
XLA Ops:
  0.0 38.2 %shard_map.118 = bf16[16,1024]{1,0:T(8,128)(2,1)S(1)} custom-call(bf16[16,1024]{1,0:T(8,128)(2,1)} %query_hbm.1, bf16[16,128]{1,0:T(8,128)(2,1)} %new_key_hbm.1, bf16[16,128]{1,0:T(8,128)(2,1)} %new_value_hbm.1, bf16[256,128]{1,0:T(8,128)(2,1)} %key_scale_hbm.1, bf16[256,128]{1,0:T(8,128)(2,1)} %value_scale_hbm.1, s32[1,16]{1,0:T(1,128)} %bitcast.7, ...), custom_call_target="tpu_custom_call" | custom-call | tf_op jit(solution)/shard_map/pallas_call | solution.py:573
  38.2 0.6 %copy.14 = bf16[16,1024]{1,0:T(8,128)(2,1)} copy(bf16[16,1024]{1,0:T(8,128)(2,1)S(1)} %shard_map.118) | data formatting | bytes 65536

commit v7 on v6

--- a/solution.py
+++ b/solution.py
@@ -85,6 +85,7 @@
     factor,
     contexts,
     block,
+    partial,
     send_part,
     recv_part,
     local_sem,
@@ -359,12 +360,14 @@
     with jax.named_scope("e_reqwait"):
         for copy in requests_in():
             copy.wait_recv()
-    with jax.named_scope("f_attend"):
-        attend([at(*back(offset)) for offset in near])
-    with jax.named_scope("g_homesend"):
-        for offset in reversed(near[1:]):
-            home_copy(back(offset)).start()
-        home_recv[me] = home_send[me]
+    for group in (near[-12:], near[:-12]):
+        with jax.named_scope("f_attend"):
+            attend([at(*back(offset)) for offset in group])
+        with jax.named_scope("g_homesend"):
+            for offset in reversed(group):
+                if offset != (0, 0):
+                    home_copy(back(offset)).start()
+    home_recv[me] = home_send[me]
 
     with jax.named_scope("j_relay"):
         up_copy(y, 3, 0).start()
@@ -395,30 +398,34 @@
     def place(source, home):
         return source * homes + lax.rem(home, outer) // 2
 
-    def context_copy(k):
+    def half_of(ref, half):
+        return ref.at[..., pl.ds(half * middle, middle)]
+
+    def context_copy(k, half):
         return remote(
-            block,
-            contexts.at[place(core, z)],
+            half_of(block, half),
+            half_of(contexts.at[place(core, z)], half),
             send_sem.at[4],
-            context_recv.at[0],
+            context_recv.at[half],
             (at(k, 0), 2 * chip + mine),
         )
 
-    def context_relay(source, k, half):
-        spot = contexts.at[place(source, z + outer - k), :, pl.ds(half * middle, middle)]
-        return remote(spot, spot, send_sem.at[4], context_recv.at[0], (at(k, 0), part))
-
-    def contexts_in(k, count):
+    def contexts_in(half, count):
+        blocks = half_of(contexts.at[pl.ds(0, count)], half)
+        return remote(blocks, blocks, send_sem.at[4], context_recv.at[half], (me, other))
+
+    def contexts_out(count):
         blocks = contexts.at[pl.ds(0, count)]
-        return remote(blocks, blocks, send_sem.at[4], context_recv.at[k], (me, other))
+        return remote(blocks, blocks, send_sem.at[4], context_recv.at[0], (me, other))
 
     with jax.named_scope("m_ctxsend"):
-        for k in (4, 3, 5, 2, 6, 1, 7):
-            context_copy(k).start()
-
-        @pl.when(mine != core)
-        def _():
-            context_copy(0).start()
+        for half in range(2):
+            for k in (4, 3, 5, 2, 6, 1, 7):
+                context_copy(k, half).start()
+
+            @pl.when(mine != core)
+            def _():
+                context_copy(0, half).start()
 
         @pl.when(mine == core)
         def _():
@@ -431,15 +438,14 @@
             down_copy(y_up, q, 0).wait_recv()
             over_copy(2, y_up, q).start()
 
-    with jax.named_scope("o_ctxwait"):
-
+    def context_wait(half):
         @pl.when(mine == core)
         def _():
-            contexts_in(0, 7).wait_recv()
+            contexts_in(half, 2 * homes - 1).wait_recv()
 
         @pl.when(mine != core)
         def _():
-            contexts_in(0, 2 * homes).wait_recv()
+            contexts_in(half, 2 * homes).wait_recv()
 
     shift = lax.rem(z + core, 2)
 
@@ -465,22 +471,51 @@
 
     order = (y, y_down, y_up, y_far)
 
+    def half_sum(column, half):
+        total = jnp.zeros((homes * rows, columns), f32)
+        for q in range(half * QUARTERS // 2, (half + 1) * QUARTERS // 2):
+            lanes = slice(q * quarter, (q + 1) * quarter)
+            for source, weight in ((core, weights_in), (1 - core, weights_over)):
+                piece = contexts[pl.ds(source * homes, homes), :, lanes]
+                total = total + dot(
+                    piece.reshape(homes * rows, quarter), weight[column, q]
+                )
+        return total
+
+    def far_sum(column):
+        total = jnp.zeros((homes * rows, columns), f32)
+        for source, weight in ((core, weights_in), (1 - core, weights_over)):
+            if weight is weights_over:
+                over_in(inner - 1, column).wait_recv()
+            for q in range(QUARTERS):
+                piece = contexts[
+                    pl.ds(source * homes, homes), :, q * quarter : (q + 1) * quarter
+                ]
+                total = total + dot(
+                    piece.reshape(homes * rows, quarter), weight[column, q]
+                )
+        return total
+
+    with jax.named_scope("o_ctxwait"):
+        context_wait(0)
+    with jax.named_scope("o_first"):
+        for n, column in enumerate(order[:-1]):
+            over_in(n, column).wait_recv()
+            partial[n] = half_sum(column, 0)
+    with jax.named_scope("o_ctxwait2"):
+        context_wait(1)
     with jax.named_scope("p_project"):
-        direct = contexts[pl.ds(core * homes, homes)].reshape(homes * rows, query_width)
-        over = contexts[pl.ds((1 - core) * homes, homes)].reshape(homes * rows, query_width)
         for n, column in enumerate(order):
-            if n == 3:
+            if n == 2:
                 for m in (0, 1):
                     up_copy(y_far, m, 1).wait_recv()
                     over_copy(3, y_far, m).start()
                     down_copy(y_far, m + 2, 1).wait_recv()
                     over_copy(3, y_far, m + 2).start()
-            over_in(n, column).wait_recv()
-            summed = jnp.zeros((homes * rows, columns), f32)
-            for q in range(QUARTERS):
-                depth = slice(q * quarter, (q + 1) * quarter)
-                summed = summed + dot(direct[:, depth], weights_in[column, q])
-                summed = summed + dot(over[:, depth], weights_over[column, q])
+            if n < inner - 1:
+                summed = partial[n] + half_sum(column, 1)
+            else:
+                summed = far_sum(column)
             send_part[column] = summed.astype(bf16).reshape(homes, rows, columns)
             for i in (2, 1, 3):
                 part_copy(n, column, i).start()
@@ -503,11 +538,11 @@
 
         @pl.when(mine == core)
         def _():
-            contexts_in(0, 2 * homes - 1).wait_send()
+            contexts_out(2 * homes - 1).wait_send()
 
         @pl.when(mine != core)
         def _():
-            contexts_in(0, 2 * homes).wait_send()
+            contexts_out(2 * homes).wait_send()
 
     with jax.named_scope("r_partwait"):
         for n, column in enumerate(order):
@@ -591,6 +626,7 @@
             pltpu.VMEM((rows, HEAD_SIZE), f32),
             pltpu.VMEM((mp, rows, query_width), bf16),
             pltpu.VMEM((rows, query_width), bf16),
+            pltpu.VMEM((inner - 1, mp // 2 * rows, columns), f32),
             pltpu.VMEM((inner, mp // 2, rows, columns), bf16),
             pltpu.VMEM((inner, mp // 2, rows, columns), bf16),
             pltpu.SemaphoreType.DMA((3,)),

time: 38.9 us -> 38.1 us (0.979)
  Pallas kernels: 38.2 us -> 37.4 us
    pallas_call x1, Pallas kernels: 38.2 us -> 37.4 us  [on_device(): pl.pallas_call(functools.partial(layer_kernel, dp, mp), out_shape=jax.Sha...]
where the time goes in v7:
time: 38.1 us; the launch traced here: 38 us
  Pallas kernels  37.4 us (98%)
  local copies, waits for them, and re-layouts  0.62 us (2%)
    pallas_call x1, Pallas kernels, on_device(): pl.pallas_call(functools.partial(layer_kernel, dp, mp), out_shape=jax.Sha...  37.4 us

profile of v7, /device:TPU:1, one launch (start us, length us, event | category | flops | bytes accessed | tf_op | source)
XLA Modules:
  0.0 38.0 jit_solution(12848054813511921710)
XLA Ops:
  0.0 37.4 %shard_map.118 = bf16[16,1024]{1,0:T(8,128)(2,1)S(1)} custom-call(bf16[16,1024]{1,0:T(8,128)(2,1)} %query_hbm.1, bf16[16,128]{1,0:T(8,128)(2,1)} %new_key_hbm.1, bf16[16,128]{1,0:T(8,128)(2,1)} %new_value_hbm.1, bf16[256,128]{1,0:T(8,128)(2,1)} %key_scale_hbm.1, bf16[256,128]{1,0:T(8,128)(2,1)} %value_scale_hbm.1, s32[1,16]{1,0:T(1,128)} %bitcast.7, ...), custom_call_target="tpu_custom_call" | custom-call | tf_op jit(solution)/shard_map/pallas_call | solution.py:608
  37.4 0.6 %copy.14 = bf16[16,1024]{1,0:T(8,128)(2,1)} copy(bf16[16,1024]{1,0:T(8,128)(2,1)S(1)} %shard_map.118) | data formatting | bytes 65536

commit v8 on v7

--- a/solution.py
+++ b/solution.py
@@ -141,11 +141,11 @@
 
     def up_copy(source, q, relay):
         piece = weights_in.at[source, q]
-        return remote(piece, piece, send_sem.at[2], weight_recv.at[relay, 0, q], (up, part))
+        return remote(piece, piece, send_sem.at[2], weight_recv.at[q + 4 * relay], (up, part))
 
     def down_copy(source, q, relay):
         piece = weights_in.at[source, q]
-        return remote(piece, piece, send_sem.at[2], weight_recv.at[relay, 1, q], (down, part))
+        return remote(piece, piece, send_sem.at[2], weight_recv.at[6 + q + 2 * relay], (down, part))
 
     def over_copy(k, source, q):
         return remote(
@@ -301,8 +301,6 @@
         down_copy(y, 2, 0).start()
         up_copy(y, 1, 0).start()
         down_copy(y, 3, 0).start()
-        up_copy(y, 2, 0).start()
-        down_copy(y, 0, 0).start()
         for q in range(QUARTERS):
             over_copy(0, y, q).start()
         fetches[1].wait()
@@ -370,6 +368,8 @@
     home_recv[me] = home_send[me]
 
     with jax.named_scope("j_relay"):
+        up_copy(y, 2, 0).start()
+        down_copy(y, 0, 0).start()
         up_copy(y, 3, 0).start()
         down_copy(y, 1, 0).start()
         for q in (0, 1):
@@ -506,7 +506,7 @@
         context_wait(1)
     with jax.named_scope("p_project"):
         for n, column in enumerate(order):
-            if n == 2:
+            if n == 3:
                 for m in (0, 1):
                     up_copy(y_far, m, 1).wait_recv()
                     over_copy(3, y_far, m).start()
@@ -533,7 +533,7 @@
             copy.wait_send()
         homes_in().wait_send()
         three = weights_in.at[pl.ds(0, inner - 1)]
-        remote(three, three, send_sem.at[2], weight_recv.at[0, 0, 0], (me, other)).wait_send()
+        remote(three, three, send_sem.at[2], weight_recv.at[0], (me, other)).wait_send()
         remote(weights_in, weights_over, send_sem.at[3], over_recv.at[0], (me, other)).wait_send()
 
         @pl.when(mine == core)
@@ -634,7 +634,7 @@
             pltpu.SemaphoreType.DMA((7,)),
             pltpu.SemaphoreType.DMA((2,)),
             pltpu.SemaphoreType.DMA((1,)),
-            pltpu.SemaphoreType.DMA((2, 2, QUARTERS)),
+            pltpu.SemaphoreType.DMA((12,)),
             pltpu.SemaphoreType.DMA((inner,)),
             pltpu.SemaphoreType.DMA((3,)),
             pltpu.SemaphoreType.DMA((inner,)),

time: 38.1 us -> 37.9 us (level)
  no operation moved by 1% of the time
where the time goes in v8:
time: 37.9 us; the launch traced here: 37.8 us
  Pallas kernels  37.2 us (98%)
  local copies, waits for them, and re-layouts  0.62 us (2%)
    pallas_call x1, Pallas kernels, on_device(): pl.pallas_call(functools.partial(layer_kernel, dp, mp), out_shape=jax.Sha...  37.2 us

profile of v8, /device:TPU:1, one launch (start us, length us, event | category | flops | bytes accessed | tf_op | source)
XLA Modules:
  0.0 37.8 jit_solution(15714429133929878277)
XLA Ops:
  0.0 37.2 %shard_map.118 = bf16[16,1024]{1,0:T(8,128)(2,1)S(1)} custom-call(bf16[16,1024]{1,0:T(8,128)(2,1)} %query_hbm.1, bf16[16,128]{1,0:T(8,128)(2,1)} %new_key_hbm.1, bf16[16,128]{1,0:T(8,128)(2,1)} %new_value_hbm.1, bf16[256,128]{1,0:T(8,128)(2,1)} %key_scale_hbm.1, bf16[256,128]{1,0:T(8,128)(2,1)} %value_scale_hbm.1, s32[1,16]{1,0:T(1,128)} %bitcast.7, ...), custom_call_target="tpu_custom_call" | custom-call | tf_op jit(solution)/shard_map/pallas_call | solution.py:608
  37.2 0.6 %copy.14 = bf16[16,1024]{1,0:T(8,128)(2,1)} copy(bf16[16,1024]{1,0:T(8,128)(2,1)S(1)} %shard_map.118) | data formatting | bytes 65536

commit v9 on v8

--- a/solution.py
+++ b/solution.py
@@ -398,8 +398,11 @@
     def place(source, home):
         return source * homes + lax.rem(home, outer) // 2
 
+    spans = ((0, QUARTERS - 1), (QUARTERS - 1, QUARTERS))
+
     def half_of(ref, half):
-        return ref.at[..., pl.ds(half * middle, middle)]
+        first, last = spans[half]
+        return ref.at[..., pl.ds(first * quarter, (last - first) * quarter)]
 
     def context_copy(k, half):
         return remote(
@@ -473,7 +476,7 @@
 
     def half_sum(column, half):
         total = jnp.zeros((homes * rows, columns), f32)
-        for q in range(half * QUARTERS // 2, (half + 1) * QUARTERS // 2):
+        for q in range(*spans[half]):
             lanes = slice(q * quarter, (q + 1) * quarter)
             for source, weight in ((core, weights_in), (1 - core, weights_over)):
                 piece = contexts[pl.ds(source * homes, homes), :, lanes]

time: 37.9 us -> 37.7 us (level)
  no operation moved by 1% of the time
where the time goes in v9:
time: 37.7 us
  Pallas kernels  37 us (98%)
  local copies, waits for them, and re-layouts  0.62 us (2%)
    pallas_call x1, Pallas kernels, on_device(): pl.pallas_call(functools.partial(layer_kernel, dp, mp), out_shape=jax.Sha...  37 us

profile of v9, /device:TPU:1, one launch (start us, length us, event | category | flops | bytes accessed | tf_op | source)
XLA Modules:
  0.0 37.7 jit_solution(9673420312452987275)
XLA Ops:
  0.0 37.0 %shard_map.118 = bf16[16,1024]{1,0:T(8,128)(2,1)S(1)} custom-call(bf16[16,1024]{1,0:T(8,128)(2,1)} %query_hbm.1, bf16[16,128]{1,0:T(8,128)(2,1)} %new_key_hbm.1, bf16[16,128]{1,0:T(8,128)(2,1)} %new_value_hbm.1, bf16[256,128]{1,0:T(8,128)(2,1)} %key_scale_hbm.1, bf16[256,128]{1,0:T(8,128)(2,1)} %value_scale_hbm.1, s32[1,16]{1,0:T(1,128)} %bitcast.7, ...), custom_call_target="tpu_custom_call" | custom-call | tf_op jit(solution)/shard_map/pallas_call | solution.py:611
  37.0 0.6 %copy.14 = bf16[16,1024]{1,0:T(8,128)(2,1)} copy(bf16[16,1024]{1,0:T(8,128)(2,1)S(1)} %shard_map.118) | data formatting | bytes 65536
